TPU v7x, 128 devices: a whole 4x4x4 slice. The times are simulated.
128 devices in a mesh: dp: 16 (over z, x), mp: 8 (over y, core).
Axes of the slice: x: 4, y: 4, z: 4, core: 2. Of those that a mesh axis runs over, the one named last changes fastest.
Arguments:
- tokens: bfloat16 [256, 4096], P('dp'), may hold values from -6 to 6
- norm_gain: float32 [4096], replicated, may hold values from 0.5 to 1.5
- router: bfloat16 [4096, 8], replicated, may hold values from -0.09375 to 0.09375
- w_gate: bfloat16 [8, 4096, 14336], P('mp', None, 'dp'), may hold values from -0.09375 to 0.09375
- w_up: bfloat16 [8, 4096, 14336], P('mp', None, 'dp'), may hold values from -0.09375 to 0.09375
- w_down: bfloat16 [8, 14336, 4096], P('mp', 'dp'), may hold values from -0.046875 to 0.046875
- final_gain: float32 [4096], replicated, may hold values from 0.5 to 1.5
- routes: int32 [256, 2], replicated, may hold values from 0 to 7, all different within a row; in each aligned block of 16 rows (0 to 15, 16 to 31, ...) at most 8 rows name the same one
- steer_hidden: bfloat16 [2, 256, 1024], P(None, 'dp'), may hold values from -6 to 6
- steer_query: bfloat16 [2, 256, 1024], P(None, 'dp', 'mp'), may hold values from -200 to 200
- steer_cache: bfloat16 [2, 2, 256, 64, 1024], P(None, None, 'dp', None, 'mp'), may hold values from -6 to 6
- steer_new: bfloat16 [2, 2, 256, 1024], P(None, None, 'dp', 'mp'), may hold values from -6 to 6
- cache_len: int32 [256], P('dp'), may hold values from 1 to 64
- steer_out: bfloat16 [2, 1024, 1024], P(None, 'mp'), may hold values from -0.1875 to 0.1875
- steer_gain: float32 [2, 1024], replicated, may hold values from 0.5 to 1.5
- base_head: bfloat16 [4096, 16000], P(None, ('dp', 'mp')), may hold values from -0.09375 to 0.09375
- steer_head: bfloat16 [2, 1024, 16000], P(None, None, ('dp', 'mp')), may hold values from -0.1875 to 0.1875
- inv_temp: float32 [256], replicated, may hold values from 0.5 to 40
Outputs:
- log_probs: float32 [256, 16000], P(None, ('dp', 'mp'))
Inputs may be any that keep to these rules, and one draw needn't show every extreme that they name: The two routes of a sequence differ; in every aligned block of 16 sequences (the sequences of one index of dp) no expert is named more than 8 times. Positions at and after cache_len[s] of sequence s's cache are unused.
All inputs are finite; a program needn't handle non-finite values.
Results may differ from a plain program's by a relative error of at most 0.00105.
Values may be sent and summed in bfloat16 or wider, within the bound.
A program may use at most 128 MiB of HBM per device.

v0:
```python
import math

import jax
import jax.numpy as jnp
from jax import lax
from jax.sharding import Mesh
from jax.sharding import PartitionSpec as P

HEAD_DIM = 128
MP = ("mp_0", "mp_1")
DP = ("dp_0", "dp_1")
DP_MP = ("dp_0", "dp_1", "mp_0", "mp_1")


steer_alpha = 2.0
norm_eps = 1e-05


def copy_for_each(x, axis):
    size = lax.axis_size(axis)
    return lax.all_to_all(jnp.broadcast_to(x[None], (size, *x.shape)), axis, 0, 0, tiled=True)


def over_copies(x, axis):
    everything = copy_for_each(x, axis)
    return jnp.sum(everything, axis=0)


def in_order(blocks, dim):
    blocks = jnp.moveaxis(blocks, 0, dim)
    dims = blocks.shape
    return blocks.reshape(*dims[:dim], dims[dim] * dims[dim + 1], *dims[dim + 2 :])


def gathered_copies(x, axis, dim):
    return in_order(copy_for_each(x, axis), dim)


def cut_along(x, dim, size):
    dims = x.shape
    blocks = x.reshape(*dims[:dim], size, dims[dim] // size, *dims[dim + 1 :])
    return jnp.moveaxis(blocks, dim, 0)


def sum_at_owner(x, axis, dim):
    size = lax.axis_size(axis)
    blocks = lax.all_to_all(cut_along(x, dim, size), axis, 0, 0, tiled=True)
    return jnp.sum(blocks.astype(jnp.float32), axis=0)


def taken_together(x, axis):
    everything = copy_for_each(x, axis)
    return jnp.sum(everything.astype(jnp.float32), axis=0)


def rows_first(arrays, axis, dims):
    turned = [jnp.moveaxis(a, dim, 0) for a, dim in zip(arrays, dims)]
    both = jnp.concatenate([t.reshape(len(t), -1) for t in turned], axis=1)
    filled, at, outs = (lax.all_gather(both, axis, axis=0, tiled=True), 0, [])
    for t, dim in zip(turned, dims):
        share = filled[:, at : at + t[0].size].reshape(-1, *t.shape[1:])
        outs.append(jnp.moveaxis(share, 0, dim))
        at += t[0].size
    return tuple(outs)


def collected_together(x, axis):
    leaves = jax.tree.leaves(x)
    turns = sorted(range(len(leaves)), key=lambda k: -leaves[k].size)
    width = (1, *leaves[turns[0]].shape)[-1]
    lines = [
        jnp.pad(leaves[k].reshape(-1), (0, -leaves[k].size % width)).reshape(-1, width)
        for k in turns
    ]
    both, at, found = (lax.all_gather(jnp.concatenate(lines), axis), 0, {})
    for k, line in zip(turns, lines):
        share = both[:, at : at + len(line)].reshape(len(both), -1)
        found[k] = share[:, : leaves[k].size].reshape(-1, *leaves[k].shape)
        at += len(line)
    numbers = iter(range(len(leaves)))
    return jax.tree.map(lambda _: found[next(numbers)], x)


def joined_all(x, axes, combine):
    for axis in axes:
        pieces = collected_together(x, axis)
        x = jax.tree.map(lambda part: part[0], pieces)
        for k in range(1, lax.axis_size(axis)):
            x = combine(x, jax.tree.map(lambda part: part[k], pieces))
    return x


def rms_scale(values, gain):
    mean_sq = jnp.mean(values * values, axis=-1, keepdims=True)
    return values * lax.rsqrt(mean_sq + norm_eps) * gain


def route_gates(normed, router, chosen, n_experts):
    logits = jnp.dot(normed, router, preferred_element_type=jnp.float32)
    marks = (chosen[:, :, None] == jnp.arange(n_experts, dtype=jnp.int32)[None, None, :]).astype(
        jnp.float32
    )
    picked = jnp.sum(logits[:, None, :] * marks, axis=2)
    first = 1.0 / (1.0 + jnp.exp(picked[:, 1] - picked[:, 0]))
    second = 1.0 / (1.0 + jnp.exp(picked[:, 0] - picked[:, 1]))
    return jnp.stack([first, second], axis=1)


def slot_tables(block_routes, block_gates, expert, capacity, n_experts):
    flat = block_routes.reshape(-1)
    marks = (flat[:, None] == jnp.arange(n_experts, dtype=jnp.int32)[None, :]).astype(jnp.int32)
    earlier = jnp.cumsum(marks, axis=0) - marks
    rank = jnp.sum(earlier * marks, axis=1).reshape(block_routes.shape)
    mine = block_routes == expert
    hits = (
        mine[:, :, None]
        & (rank[:, :, None] == jnp.arange(capacity, dtype=jnp.int32)[None, None, :])
    ).astype(jnp.float32)
    select = jnp.transpose(jnp.sum(hits, axis=1))
    combine = jnp.sum(hits * block_gates[:, :, None], axis=1)
    return (select, combine)


def swiglu(rows, gate_mat, up_mat):
    gate_part = jnp.dot(rows, gate_mat, preferred_element_type=jnp.float32)
    up_part = jnp.dot(rows, up_mat, preferred_element_type=jnp.float32)
    return (jax.nn.silu(gate_part) * up_part).astype(jnp.bfloat16)


def steer_attention(steer_query, steer_cache, steer_new, cache_len):
    models, seq_rows, width = steer_query.shape
    heads = width // HEAD_DIM
    span = steer_cache.shape[3]
    scale = 1.0 / math.sqrt(HEAD_DIM)
    queries = steer_query.reshape(models, seq_rows, heads, HEAD_DIM)
    keys = steer_cache[:, 0].reshape(models, seq_rows, span, heads, HEAD_DIM)
    values = steer_cache[:, 1].reshape(models, seq_rows, span, heads, HEAD_DIM)
    new_keys = steer_new[:, 0].reshape(models, seq_rows, heads, HEAD_DIM)
    new_values = steer_new[:, 1].reshape(models, seq_rows, heads, HEAD_DIM).astype(jnp.float32)
    scores = (
        jnp.einsum("mshd,msphd->mshp", queries, keys, preferred_element_type=jnp.float32) * scale
    )
    new_score = (
        jnp.einsum("mshd,mshd->msh", queries, new_keys, preferred_element_type=jnp.float32) * scale
    )
    live = (jnp.arange(span, dtype=jnp.int32)[None, :] < cache_len[:, None])[None, :, None, :]
    masked = jnp.where(live, scores, -1e30)
    summit = jnp.maximum(jnp.max(masked, axis=3), new_score)
    expo = jnp.where(live, jnp.exp(masked - summit[..., None]), 0.0)
    new_expo = jnp.exp(new_score - summit)
    denom = jnp.sum(expo, axis=3) + new_expo
    weights = (expo / denom[..., None]).astype(jnp.bfloat16)
    new_weight = (new_expo / denom).astype(jnp.bfloat16).astype(jnp.float32)
    attended = jnp.einsum("mshp,msphd->mshd", weights, values, preferred_element_type=jnp.float32)
    attended = attended + new_weight[..., None] * new_values
    return attended.reshape(models, seq_rows, width).astype(jnp.bfloat16)


def merge_pair(first, second):
    summit = jnp.maximum(first[0], second[0])
    return (summit, first[1] * jnp.exp(first[0] - summit) + second[1] * jnp.exp(second[0] - summit))


def per_device(
    tokens,
    norm_gain,
    router,
    w_gate,
    w_up,
    w_down,
    final_gain,
    routes,
    steer_hidden,
    steer_query,
    steer_cache,
    steer_new,
    cache_len,
    steer_out,
    steer_gain,
    base_head,
    steer_head,
    inv_temp,
):
    n_experts = lax.axis_size(MP)
    expert = lax.axis_index(MP)
    seq_rows = tokens.shape[0]
    capacity = 4 * seq_rows // n_experts
    gate_mat = w_gate[0]
    up_mat = w_up[0]
    down_mat = w_down[0]
    attended = steer_attention(steer_query, steer_cache, steer_new, cache_len)
    proj = jnp.einsum("msw,mwv->msv", attended, steer_out, preferred_element_type=jnp.float32)
    proj = over_copies(proj, MP)
    steer_state = steer_hidden.astype(jnp.float32) + proj
    steer_normed = rms_scale(steer_state, steer_gain[:, None, :]).astype(jnp.bfloat16)
    resid = tokens.astype(jnp.float32)
    normed = rms_scale(resid, norm_gain).astype(jnp.bfloat16)
    first_row = lax.axis_index(DP) * seq_rows
    own_routes = lax.dynamic_slice_in_dim(routes, first_row, seq_rows, 0)
    gates = route_gates(normed, router, own_routes, n_experts)
    select, combine = slot_tables(own_routes, gates, expert, capacity, n_experts)
    slot_in = jnp.dot(
        select.astype(jnp.bfloat16), normed, preferred_element_type=jnp.float32
    ).astype(jnp.bfloat16)
    hidden = swiglu(gathered_copies(slot_in, DP, 0), gate_mat, up_mat)
    slot_out = sum_at_owner(
        jnp.dot(hidden, down_mat, preferred_element_type=jnp.float32).astype(jnp.bfloat16), DP, 0
    )
    mixed = jnp.dot(combine, slot_out, precision=lax.Precision.HIGHEST)
    moe = taken_together(mixed.astype(jnp.bfloat16), MP).astype(jnp.float32)
    base_normed = rms_scale(resid + moe, final_gain).astype(jnp.bfloat16)
    base_all, steer_all = rows_first((base_normed[None], steer_normed), DP, (1, 1))
    base_all = base_all[0]
    base_logits = jnp.dot(base_all, base_head, preferred_element_type=jnp.float32)
    plus = jnp.dot(steer_all[0], steer_head[0], preferred_element_type=jnp.float32)
    minus = jnp.dot(steer_all[1], steer_head[1], preferred_element_type=jnp.float32)
    combined = inv_temp[:, None] * (base_logits + steer_alpha * (plus - minus))
    local_peak = jnp.max(combined, axis=1)
    local_total = jnp.sum(jnp.exp(combined - local_peak[:, None]), axis=1)
    peak_val, total = joined_all((local_peak, local_total), DP_MP, merge_pair)
    return combined - peak_val[:, None] - jnp.log(total)[:, None]


def solution(mesh):
    finer = Mesh(mesh.devices.reshape(4, 4, 4, 2), ("dp_0", "dp_1", "mp_0", "mp_1"))
    placed = (
        P(DP, None),
        P(),
        P(),
        P(MP, None, DP),
        P(MP, None, DP),
        P(MP, DP, None),
        P(),
        P(),
        P(None, DP, None),
        P(None, DP, MP),
        P(None, None, DP, None, MP),
        P(None, None, DP, MP),
        P(DP),
        P(None, MP, None),
        P(),
        P(None, DP_MP),
        P(None, None, DP_MP),
        P(),
    )
    return jax.shard_map(
        per_device, mesh=finer, in_specs=placed, out_specs=P(None, DP_MP), check_vma=False
    )
```

profile of v0, /device:TPU:1, one launch (start us, length us, event | category | flops | bytes accessed | tf_op | source)
XLA Modules:
  0.0 206.8 jit_solution(15885888711797221466)
XLA Ops:
  6.5 1.1 fusion.41
  7.7 0.8 broadcast_compare_fusion
  8.5 1.1 fusion.49
  9.7 0.1 eq.51
  9.9 0.2 select_reduce_fusion
  10.2 0.1 copy.57
  10.3 1.1 convolution_convert_fusion.1
  11.5 1.1 broadcast_in_dim.24
  12.6 8.4 %all-to-all-start = ((bf16[16,8,4096]{2,1,0:T(8,128)(2,1)}), bf16[16,8,4096]{2,1,0:T(8,128)(2,1)S(1)}, u32[]{:S(2)}, u32[]{:S(2)}) async-start(bf16[16,8,4096]{2,1,0:T(8,128)(2,1)} %broadcast_in_dim.24), calls=%async_computation | async-start | bytes 2097152 | tf_op jit(solution)/shard_map/all_to_all | solution.py:21
  21.0 0.8 fusion.53
  21.8 0.7 iota_compare_fusion.1
  22.5 1.4 fusion.32
  24.0 13.0 %all-to-all-done = bf16[16,8,4096]{2,1,0:T(8,128)(2,1)S(1)} async-done(((bf16[16,8,4096]{2,1,0:T(8,128)(2,1)}), bf16[16,8,4096]{2,1,0:T(8,128)(2,1)S(1)}, u32[]{:S(2)}, u32[]{:S(2)}) %all-to-all-start) | async-done | bytes 1048608 | tf_op jit(solution)/shard_map/all_to_all | solution.py:21
  37.0 4.3 %fusion.4 = f32[128,896]{1,0:T(8,128)S(1)} fusion(bf16[1,4096,896]{2,1,0:T(8,128)(2,1)} %param.21, bf16[16,8,4096]{2,1,0:T(8,128)(2,1)S(1)} %all-to-all-done), kind=kOutput, calls=%fused_computation.4 | convolution fusion | flops 939524096 | bytes 8847360 | tf_op jit(solution)/shard_map/dot_general | solution.py:125
  41.4 8.6 %fusion.9 = bf16[16,8,4096]{2,1,0:T(8,128)(2,1)} fusion(bf16[1,896,4096]{2,1,0:T(8,128)(2,1)} %param.23, bf16[1,4096,896]{2,1,0:T(8,128)(2,1)} %param.22, bf16[16,8,4096]{2,1,0:T(8,128)(2,1)S(1)} %all-to-all-done, f32[128,896]{1,0:T(8,128)S(1)} %fusion.4), kind=kOutput, calls=%fused_computation.7 | convolution fusion | flops 1880260608 | bytes 17235968 | tf_op jit(solution)/shard_map/dot_general | solution.py:207
  50.1 4.3 %all-to-all-start.1 = ((bf16[16,8,4096]{2,1,0:T(8,128)(2,1)}), bf16[16,8,4096]{2,1,0:T(8,128)(2,1)S(1)}, u32[]{:S(2)}, u32[]{:S(2)}) async-start(bf16[16,8,4096]{2,1,0:T(8,128)(2,1)} %fusion.9), calls=%async_computation.1 | async-start | bytes 2097152 | tf_op jit(solution)/shard_map/all_to_all | solution.py:47
  54.4 0.2 fusion.58
  54.6 0.1 fusion.64
  54.7 1.3 fusion.30
  56.0 0.2 fusion.59
  56.2 13.3 %all-to-all-done.1 = bf16[16,8,4096]{2,1,0:T(8,128)(2,1)S(1)} async-done(((bf16[16,8,4096]{2,1,0:T(8,128)(2,1)}), bf16[16,8,4096]{2,1,0:T(8,128)(2,1)S(1)}, u32[]{:S(2)}, u32[]{:S(2)}) %all-to-all-start.1) | async-done | bytes 1048608 | tf_op jit(solution)/shard_map/all_to_all | solution.py:47
  69.6 1.1 broadcast_in_dim.29
  70.7 7.7 %all-to-all-start.3 = ((f32[8,2,16,1024]{3,2,1,0:T(8,128)}), f32[8,2,16,1024]{3,2,1,0:T(8,128)S(1)}, u32[]{:S(2)}, u32[]{:S(2)}) async-start(f32[8,2,16,1024]{3,2,1,0:T(8,128)} %broadcast_in_dim.29), calls=%async_computation.3 | async-start | bytes 2097152 | tf_op jit(solution)/shard_map/all_to_all | solution.py:21
  78.3 0.1 convert_reduce_fusion.1
  78.5 0.4 convolution_convert_fusion
  78.9 14.4 %all-to-all-done.3 = f32[8,2,16,1024]{3,2,1,0:T(8,128)S(1)} async-done(((f32[8,2,16,1024]{3,2,1,0:T(8,128)}), f32[8,2,16,1024]{3,2,1,0:T(8,128)S(1)}, u32[]{:S(2)}, u32[]{:S(2)}) %all-to-all-start.3) | async-done | bytes 1048608 | tf_op jit(solution)/shard_map/all_to_all | solution.py:21
  93.3 1.1 broadcast_in_dim.25
  94.4 4.4 %all-to-all-start.2 = ((bf16[8,16,4096]{2,1,0:T(8,128)(2,1)}), bf16[8,16,4096]{2,1,0:T(8,128)(2,1)S(1)}, u32[]{:S(2)}, u32[]{:S(2)}) async-start(bf16[8,16,4096]{2,1,0:T(8,128)(2,1)} %broadcast_in_dim.25), calls=%async_computation.2 | async-start | bytes 2097152 | tf_op jit(solution)/shard_map/all_to_all | solution.py:21
  98.9 0.1 multiply_reduce_fusion.1
  99.1 14.7 %all-to-all-done.2 = bf16[8,16,4096]{2,1,0:T(8,128)(2,1)S(1)} async-done(((bf16[8,16,4096]{2,1,0:T(8,128)(2,1)}), bf16[8,16,4096]{2,1,0:T(8,128)(2,1)S(1)}, u32[]{:S(2)}, u32[]{:S(2)}) %all-to-all-start.2) | async-done | bytes 1048608 | tf_op jit(solution)/shard_map/all_to_all | solution.py:21
  113.8 0.1 convert_reduce_fusion
  114.0 0.2 multiply_reduce_fusion
  114.1 0.1 multiply_convert_fusion
  114.2 0.7 pad_maximum_fusion
  115.0 2.1 %fusion.109 = (bf16[1,1024,125]{1,0,2:T(2,128)(2,1)S(1)}, bf16[1,1024,125]{1,0,2:T(2,128)(2,1)S(1)}) fusion(bf16[2,1024,125]{1,0,2:T(2,128)(2,1)} %param.34), kind=kLoop, calls=%fused_computation.162 | loop fusion | bytes 1024000 | tf_op jit(solution)/shard_map/slice | solution.py:216
  117.1 0.5 copy.75
  117.5 1.1 copy.74
  118.6 39.7 %all-gather.10.cloned.1.call-done = bf16[256,6144]{1,0:T(8,128)(2,1)} async-done(((bf16[16,6144]{1,0:T(8,128)(2,1)}), bf16[256,6144]{1,0:T(8,128)(2,1)}) %all-gather.10.cloned.1.call-update) | async-done | bytes 3145744 | tf_op jit(solution)/shard_map/all_gather | solution.py:59
  158.4 1.3 slice.227
  159.6 0.5 copy.73
  160.2 1.2 fusion.29
  161.4 2.4 %fusion.12 = f32[256,125]{0,1:T(8,128)S(1)} fusion(bf16[4096,125]{1,0:T(8,128)(2,1)S(1)} %copy-done, bf16[256,6144]{1,0:T(8,128)(2,1)} %all-gather.10.cloned.1.call-done), kind=kOutput, calls=%fused_computation.10 | convolution fusion | flops 262144000 | bytes 3249152 | tf_op jit(solution)/shard_map/dot_general | solution.py:214
  163.8 0.3 fusion.111
  164.2 8.1 %all-gather.4 = f32[4,2,256]{2,1,0:T(2,128)S(1)} all-gather(f32[1,2,256]{2,1,0:T(2,128)S(1)} %maximum_bitcast_fusion), channel_id=2, replica_groups=mesh['dp_0'=4,'dp_1'=4,'mp_0'=4,'mp_1'=2] {'dp_0'}, dimensions={0}, use_global_device_ids=true | all-gather | bytes 10240 | tf_op jit(solution)/shard_map/all_gather | solution.py:75
  172.4 8.1 %all-gather.5 = f32[4,2,256]{2,1,0:T(2,128)S(1)} all-gather(f32[1,2,256]{2,1,0:T(2,128)S(1)} %maximum_bitcast_fusion.1), channel_id=3, replica_groups=mesh['dp_0'=4,'dp_1'=4,'mp_0'=4,'mp_1'=2] {'dp_1'}, dimensions={0}, use_global_device_ids=true | all-gather | bytes 10240 | tf_op jit(solution)/shard_map/all_gather | solution.py:75
  180.6 8.5 %all-gather.6 = f32[4,2,256]{2,1,0:T(2,128)S(1)} all-gather(f32[1,2,256]{2,1,0:T(2,128)S(1)} %maximum_bitcast_fusion.2), channel_id=4, replica_groups=mesh['dp_0'=4,'dp_1'=4,'mp_0'=4,'mp_1'=2] {'mp_0'}, dimensions={0}, use_global_device_ids=true | all-gather | bytes 10240 | tf_op jit(solution)/shard_map/all_gather | solution.py:75
  189.1 10.1 %all-gather.7 = f32[2,2,256]{2,1,0:T(2,128)S(1)} all-gather(f32[1,2,256]{2,1,0:T(2,128)S(1)} %maximum_bitcast_fusion.3), channel_id=5, replica_groups=mesh['dp_0'=4,'dp_1'=4,'mp_0'=4,'mp_1'=2] {'mp_1'}, dimensions={0}, use_global_device_ids=true | all-gather | bytes 6144 | tf_op jit(solution)/shard_map/all_gather | solution.py:75
  199.2 0.8 copy.64
  (46 shorter events, 0.9 us)
Async XLA Ops:
  6.5 154.9 %copy-start = (bf16[4096,125]{1,0:T(8,128)(2,1)S(1)}, bf16[4096,125]{1,0:T(8,128)(2,1)}, u32[]{:S(2)}) copy-start(bf16[4096,125]{1,0:T(8,128)(2,1)} %param.33) | copy-start | bytes 3072004
  12.6 24.5 %all-to-all-start = ((bf16[16,8,4096]{2,1,0:T(8,128)(2,1)}), bf16[16,8,4096]{2,1,0:T(8,128)(2,1)S(1)}, u32[]{:S(2)}, u32[]{:S(2)}) async-start(bf16[16,8,4096]{2,1,0:T(8,128)(2,1)} %broadcast_in_dim.24), calls=%async_computation | async-start | bytes 2097152 | tf_op jit(solution)/shard_map/all_to_all | solution.py:21
  41.4 14.6 %copy-start.2 = (bf16[2,128,1024]{2,1,0:T(8,128)(2,1)S(1)}, bf16[2,128,1024]{2,1,0:T(8,128)(2,1)}, u32[]{:S(2)}) copy-start(bf16[2,128,1024]{2,1,0:T(8,128)(2,1)} %param.31) | copy-start | bytes 1572868
  41.4 14.6 %copy-start.4 = (bf16[2,2,16,128]{3,2,1,0:T(8,128)(2,1)S(1)}, bf16[2,2,16,128]{3,2,1,0:T(8,128)(2,1)}, u32[]{:S(2)}) copy-start(bf16[2,2,16,128]{3,2,1,0:T(8,128)(2,1)} %param.29) | copy-start | bytes 49156
  50.0 48.8 %copy-start.3 = (bf16[2,16,1024]{2,1,0:T(8,128)(2,1)S(1)}, bf16[2,16,1024]{2,1,0:T(8,128)(2,1)}, u32[]{:S(2)}) copy-start(bf16[2,16,1024]{2,1,0:T(8,128)(2,1)} %param.26) | copy-start | bytes 196612
  50.0 49.0 %copy-start.6 = (f32[2,1024]{1,0:T(2,128)S(1)}, f32[2,1024]{1,0:T(2,128)}, u32[]{:S(2)}) copy-start(f32[2,1024]{1,0:T(2,128)} %param.32) | copy-start | bytes 24580
  50.0 63.9 %copy-start.1 = (bf16[16,4096]{1,0:T(8,128)(2,1)S(1)}, bf16[16,4096]{1,0:T(8,128)(2,1)}, u32[]{:S(2)}) copy-start(bf16[16,4096]{1,0:T(8,128)(2,1)} %param.18) | copy-start | bytes 393220
  50.0 64.1 %copy-start.5 = (f32[4096]{0:T(1024)S(1)}, f32[4096]{0:T(1024)}, u32[]{:S(2)}) copy-start(f32[4096]{0:T(1024)} %param.24) | copy-start | bytes 49156
  50.1 19.5 %all-to-all-start.1 = ((bf16[16,8,4096]{2,1,0:T(8,128)(2,1)}), bf16[16,8,4096]{2,1,0:T(8,128)(2,1)S(1)}, u32[]{:S(2)}, u32[]{:S(2)}) async-start(bf16[16,8,4096]{2,1,0:T(8,128)(2,1)} %fusion.9), calls=%async_computation.1 | async-start | bytes 2097152 | tf_op jit(solution)/shard_map/all_to_all | solution.py:47
  70.7 22.6 %all-to-all-start.3 = ((f32[8,2,16,1024]{3,2,1,0:T(8,128)}), f32[8,2,16,1024]{3,2,1,0:T(8,128)S(1)}, u32[]{:S(2)}, u32[]{:S(2)}) async-start(f32[8,2,16,1024]{3,2,1,0:T(8,128)} %broadcast_in_dim.29), calls=%async_computation.3 | async-start | bytes 2097152 | tf_op jit(solution)/shard_map/all_to_all | solution.py:21
  94.4 19.4 %all-to-all-start.2 = ((bf16[8,16,4096]{2,1,0:T(8,128)(2,1)}), bf16[8,16,4096]{2,1,0:T(8,128)(2,1)S(1)}, u32[]{:S(2)}, u32[]{:S(2)}) async-start(bf16[8,16,4096]{2,1,0:T(8,128)(2,1)} %broadcast_in_dim.25), calls=%async_computation.2 | async-start | bytes 2097152 | tf_op jit(solution)/shard_map/all_to_all | solution.py:21
  98.8 59.5 %all-gather.10.cloned.1.call-start = ((), (), s32[]{:S(2)}) async-start(), calls=%async_computation.4 | async-start | bytes 3342336 | tf_op jit(solution)/shard_map/all_gather | solution.py:59
  99.1 64.7 %copy-start.7 = (f32[256]{0:T(256)S(1)}, f32[256]{0:T(256)}, u32[]{:S(2)}) copy-start(f32[256]{0:T(256)} %param.35) | copy-start | bytes 3076
Sparse Core Ops, SparseCore 0:
  115.1 43.2 all-gather.9
where the time goes:
time: 208 us; the launch traced here: 207 us
  waiting for transfers between devices  95.2 us (46%)
  blocking collectives  34.8 us (17%)
  starting transfers between devices  24.8 us (12%)
  matrix products  22.5 us (11%)
  between operations  13.7 us (7%)
  local copies, waits for them, and re-layouts  9.92 us (5%)
  other arithmetic  5.86 us (3%)
    all_to_all x3, waiting for transfers between devices, copy_for_each(): lax.all_to_all(jnp.broadcast_to(x[None], (size, *x.shape)), axis, 0, 0, t...  42.1 us
    all_gather x1, waiting for transfers between devices, rows_first(): filled, at, outs = (lax.all_gather(both, axis, axis=0, tiled=True), 0, [])  39.7 us
    all_gather x4, blocking collectives, collected_together(): both, at, found = (lax.all_gather(jnp.concatenate(lines), axis), 0, {})  34.8 us
    all_to_all x3, starting transfers between devices, copy_for_each(): lax.all_to_all(jnp.broadcast_to(x[None], (size, *x.shape)), axis, 0, 0, t...  20.5 us
    all_to_all x1, waiting for transfers between devices, sum_at_owner(): blocks = lax.all_to_all(cut_along(x, dim, size), axis, 0, 0, tiled=True)  13.3 us
    dot_general x1, matrix products, per_device(): jnp.dot(hidden, down_mat, preferred_element_type=jnp.float32)  8.64 us
    all_to_all x1, starting transfers between devices, sum_at_owner(): blocks = lax.all_to_all(cut_along(x, dim, size), axis, 0, 0, tiled=True)  4.35 us
    dot_general x1, matrix products, swiglu(): gate_part = jnp.dot(rows, gate_mat, preferred_element_type=jnp.float32)  4.34 us
  transfers between devices with their start and end apart: 5, of which 5 were waited for; matrix products, arithmetic and copies ran while one was open for 5% of the time, Pallas kernels for 0%

commit v1 on v0

v1 whole, which is shorter than its diff:
```python
import functools
import math

import jax
import jax.numpy as jnp
from jax import lax
from jax.experimental import pallas as pl
from jax.experimental.pallas import tpu as pltpu
from jax.sharding import PartitionSpec as P

F32 = jnp.float32
BF16 = jnp.bfloat16
EPS = 1e-5
ALPHA = 2.0
HEAD_DIM = 128
NC = 4
WC = 4


def iota(shape, dim):
    return lax.broadcasted_iota(jnp.int32, shape, dim)


def eye(rows, cols):
    return iota((rows, cols), 0) == iota((rows, cols), 1)


def to_col(row, rows):
    n = row.shape[1]
    return jnp.sum(jnp.where(eye(rows, n), row, 0.0), axis=1, keepdims=True)


def to_row(col, cols):
    n = col.shape[0]
    return jnp.sum(jnp.where(eye(n, cols), col, 0.0), axis=0, keepdims=True)


def nt(a, b):
    return lax.dot_general(a, b, (((1,), (1,)), ((), ())), preferred_element_type=F32)


def mm(a, b):
    return jnp.dot(a, b, preferred_element_type=F32)


def kernel(
    tokens_h, norm_gain_h, router_h, w_gate_h, w_up_h, w_down_h, final_gain_h, routes_h,
    hidden_h, query_h, cache_h, new_h, len_h, sout_h, sgain_h, bhead_h, shead_h, temp_h,
    out_ref,
    tokens, norm_gain, router, w_gate, w_up, w_down, final_gain, routes,
    hidden, query, cache, new, clen, sout, sgain, bhead, shead, temp,
    xs, xr, act, pbuf, prec, stbuf, sall, rsend, rrecv, msend, mrecv,
    xa, xb, sq1, sq2, sqs, lsend, l1, l2, slog, comb_s,
    lsem, bsem_s, bsem_r,
):
    dp = lax.axis_index("dp")
    mp = lax.axis_index("mp")
    y, c = mp // 2, mp % 2
    z, x = dp // 4, dp % 4

    dp_peers = [
        (lax.rem(z + k // 4, 4) * 4 + lax.rem(x + k % 4, 4), mp)
        for k in (1, 3, 4, 12, 5, 7, 13, 15, 2, 8, 6, 14, 9, 11, 10)
    ]
    dp_slot = (1, 3, 4, 12, 5, 7, 13, 15, 2, 8, 6, 14, 9, 11, 10)
    def dp_from(k):
        return (lax.rem(z + 4 - k // 4, 4) * 4 + lax.rem(x + 4 - k % 4, 4), mp)

    mp_peers = [(dp, lax.rem(mp + k, 8)) for k in range(1, 8)]
    y_peers = [(dp, lax.rem(y + k, 4) * 2 + c) for k in (1, 3, 2)]
    sibling = (dp, y * 2 + 1 - c)

    def rcopy(src, dst, phase, dev):
        return pltpu.make_async_remote_copy(
            src_ref=src, dst_ref=dst, send_sem=bsem_s.at[phase], recv_sem=bsem_r.at[phase],
            device_id=dev, device_id_type=pl.DeviceIdType.MESH,
        )

    pending = []

    def send(src, dst, phase, dev):
        rcopy(src, dst, phase, dev).start()

    def wait_in(ref, phase):
        rcopy(ref, ref, phase, sibling).wait_recv()

    def sent(ref, phase):
        pending.append((ref, phase))

    (X, PR, ST, S1, S2, S3, M, A1, A2, A3, B1, B2, B3, Q1, Q2, L1, L2) = range(17)
    R0 = 17

    pairs = [
        (tokens_h, tokens), (norm_gain_h, norm_gain), (routes_h, routes), (router_h, router),
        (query_h, query), (cache_h, cache), (new_h, new), (len_h, clen), (sout_h, sout),
        (hidden_h, hidden), (sgain_h, sgain),
        (final_gain_h, final_gain), (temp_h, temp),
    ]
    late = [(w_down_h.at[0], w_down), (shead_h, shead), (bhead_h, bhead)]
    copies = {}

    def fetch(src, dst, n):
        cp = pltpu.make_async_copy(src, dst, lsem.at[n])
        cp.start()
        return cp

    n = 0
    for src, dst in pairs:
        copies[id(dst)] = fetch(src, dst, n)
        n += 1
    barrier = pltpu.get_barrier_semaphore()
    for dev in dp_peers + mp_peers:
        pl.semaphore_signal(barrier, inc=1, device_id=dev, device_id_type=pl.DeviceIdType.MESH)
    wcopies = []
    kw = w_gate.shape[0] // WC
    for i in range(WC):
        rows = pl.ds(i * kw, kw)
        wcopies.append(fetch(w_gate_h.at[0, rows], w_gate.at[rows], n))
        wcopies.append(fetch(w_up_h.at[0, rows], w_up.at[rows], n + 1))
        n += 2
    for src, dst in late:
        copies[id(dst)] = fetch(src, dst, n)
        n += 1

    def need(*refs):
        for r in refs:
            copies[id(r)].wait()

    need(tokens, norm_gain, routes)
    tok = tokens[...].astype(F32)
    mean_sq = jnp.mean(tok * tok, axis=1, keepdims=True)
    normed = (tok * lax.rsqrt(mean_sq + EPS) * norm_gain[...]).astype(BF16)
    rt = routes[...]
    lanes = iota((16, 256), 1)
    own = lanes == dp * 16 + iota((16, 256), 0)
    earlier = (lanes >= dp * 16) & (lanes < dp * 16 + iota((16, 256), 0))
    rt0, rt1 = rt[0:1, :], rt[1:2, :]
    hit_all = ((rt0 == mp) | (rt1 == mp)).astype(F32)
    r0 = jnp.sum(jnp.where(own, rt0.astype(F32), 0.0), axis=1, keepdims=True)
    r1 = jnp.sum(jnp.where(own, rt1.astype(F32), 0.0), axis=1, keepdims=True)
    hit = jnp.sum(jnp.where(own, hit_all, 0.0), axis=1, keepdims=True)
    rank = jnp.sum(jnp.where(earlier, hit_all, 0.0), axis=1, keepdims=True)
    hit_row = jnp.sum(jnp.where(eye(16, 128), hit, 0.0), axis=0, keepdims=True)
    rank_row = jnp.sum(
        jnp.where(iota((16, 128), 0) < iota((16, 128), 1), hit, 0.0), axis=0, keepdims=True
    )
    select = jnp.where(
        (hit_row > 0.5) & (rank_row == iota((8, 128), 0).astype(F32)), 1.0, 0.0
    )[:, :16].astype(BF16)
    slot_in = mm(select, normed).astype(BF16)
    xs[...] = slot_in
    xr[0] = slot_in

    pl.semaphore_wait(barrier, 22)
    for k, dev in zip(dp_slot, dp_peers):
        send(xs, xr.at[k], X, dev)
    sent(xr.at[pl.ds(0, 15)], X)

    need(query, cache, new, clen, sout)
    len_col = to_col(clen[...].astype(F32), 16).astype(jnp.int32)
    pos = iota((16, 1024), 1) - 64 * iota((16, 1024), 0)
    live = (pos >= 0) & (pos < len_col)
    scale = 1.0 / math.sqrt(HEAD_DIM)
    for m in range(2):
        q = query[m]
        scores = nt(q, cache[m, 0].reshape(1024, 128)) * scale
        new_score = (
            jnp.sum(q.astype(F32) * new[m, 0].astype(F32), axis=1, keepdims=True) * scale
        )
        masked = jnp.where(live, scores, -1e30)
        summit = jnp.maximum(jnp.max(masked, axis=1, keepdims=True), new_score)
        expo = jnp.where(live, jnp.exp(masked - summit), 0.0)
        new_expo = jnp.exp(new_score - summit)
        denom = jnp.sum(expo, axis=1, keepdims=True) + new_expo
        weights = (expo / denom).astype(BF16)
        new_weight = (new_expo / denom).astype(BF16).astype(F32)
        att = mm(weights, cache[m, 1].reshape(1024, 128)) + new_weight * new[m, 1].astype(F32)
        proj = mm(att.astype(BF16), sout[m])
        for e in range(8):
            pbuf[e, m] = proj[:, e * 128 : (e + 1) * 128]
    for k, dev in enumerate(mp_peers):
        send(pbuf.at[dev[1]], prec.at[k], PR, dev)
    sent(prec, PR)

    need(router)
    logits = nt(normed, router[...])
    experts = iota((16, 8), 1).astype(F32)
    p0 = jnp.sum(jnp.where(experts == r0, logits, 0.0), axis=1, keepdims=True)
    p1 = jnp.sum(jnp.where(experts == r1, logits, 0.0), axis=1, keepdims=True)
    mine = mp.astype(F32)
    gate = jnp.where(
        r0 == mine,
        1.0 / (1.0 + jnp.exp(p1 - p0)),
        jnp.where(r1 == mine, 1.0 / (1.0 + jnp.exp(p0 - p1)), 0.0),
    )
    comb_s[...] = jnp.where(
        (hit > 0.5) & (rank == iota((16, 128), 1).astype(F32)), gate, 0.0
    )

    need(hidden, sgain)
    wait_in(prec, PR)
    head_cols = pl.ds(pl.multiple_of(mp * 128, 128), 128)
    state = hidden[:, :, head_cols].astype(F32) + pbuf[mp]
    for k in range(7):
        state = state + prec[k]
    stbuf[mp] = state
    for dev in mp_peers:
        send(stbuf.at[mp], stbuf.at[mp], ST, dev)
    sent(stbuf.at[pl.ds(0, 7)], ST)
    wait_in(stbuf.at[pl.ds(0, 7)], ST)
    sq_sum = jnp.zeros((16, 1), F32)
    for e in range(8):
        part = stbuf[e, c]
        sq_sum = sq_sum + jnp.sum(part * part, axis=1, keepdims=True)
    inv = lax.rsqrt(sq_sum * (1.0 / 1024.0) + EPS)
    for h in range(2):
        cols = pl.ds(pl.multiple_of(y * 256 + h * 128, 128), 128)
        both = sgain[:, cols]
        g = jnp.where(c == 0, both[0:1], both[1:2])
        sall[c, y, dp, :, h * 128 : (h + 1) * 128] = (stbuf[2 * y + h, c] * inv * g).astype(BF16)
    for dev in dp_peers:
        send(sall.at[c, y, dp], sall.at[c, y, dp], S1, dev)
    sent(sall.at[0, 0, pl.ds(0, 15)], S1)

    wait_in(xr.at[pl.ds(1, 15)], X)
    for cp in wcopies:
        cp.wait()
    kx = xr.shape[2]

    def up_tile(col, width):
        rows = xr[...].reshape(128, kx)
        g = mm(rows, w_gate[:, pl.ds(col, width)])
        u = mm(rows, w_up[:, pl.ds(col, width)])
        act[:, pl.ds(col, width)] = (g / (1.0 + jnp.exp(-g)) * u).astype(BF16)

    ff = w_gate.shape[1]
    full = ff // 256

    def up_body(i, carry):
        up_tile(pl.multiple_of(i * 256, 256), 256)
        return carry

    lax.fori_loop(0, full, up_body, 0)
    if ff % 256:
        up_tile(full * 256, ff % 256)

    wait_in(sall.at[0, 0, pl.ds(0, 15)], S1)
    for dev in y_peers:
        send(sall.at[c, y], sall.at[c, y], S2, dev)
    sent(sall.at[0, pl.ds(0, 3)], S2)

    need(w_down)
    wn = w_down.shape[1] // NC
    for q in range(NC):
        def down_body(i, carry):
            col = pl.multiple_of(q * wn + i * 256, 256)
            res = mm(act[...], w_down[:, pl.ds(col, 256)])
            rsend[q, :, :, pl.ds(pl.multiple_of(i * 256, 256), 256)] = res.reshape(
                16, 8, 256
            ).astype(BF16)
            return carry

        lax.fori_loop(0, wn // 256, down_body, 0)
        for k in dp_slot:
            send(rsend.at[q, k], rrecv.at[q, k], R0 + q, dp_from(k))
        sent(rsend.at[q, pl.ds(0, 15)], R0 + q)

    wait_in(sall.at[0, pl.ds(0, 3)], S2)
    send(sall.at[c], sall.at[c], S3, sibling)
    sent(sall.at[0], S3)
    need(shead)
    wait_in(sall.at[0], S3)
    for m in range(2):
        acc = None
        for yy in range(4):
            part = mm(sall[m, yy].reshape(256, 256), shead[m, yy * 256 : (yy + 1) * 256, :])
            acc = part if acc is None else acc + part
        if m == 0:
            slog[...] = acc
        else:
            slog[...] = ALPHA * (slog[...] - acc)

    comb = comb_s[...]
    for q in range(NC):
        wait_in(rrecv.at[q, pl.ds(1, 15)], R0 + q)
        total = rsend[q, 0].astype(F32)
        for k in range(1, 16):
            total = total + rrecv[q, k].astype(F32)
        mixed = None
        for s in range(8):
            term = comb[:, s : s + 1] * total[s : s + 1, :]
            mixed = term if mixed is None else mixed + term
        mixed = mixed.astype(BF16)
        per = wn // 512
        for h in range(per):
            msend[q * per + h] = mixed[:, h * 512 : (h + 1) * 512]
    for k, dev in enumerate(mp_peers):
        send(msend.at[dev[1]], mrecv.at[k], M, dev)
    sent(mrecv, M)
    need(final_gain)
    mine_cols = pl.ds(pl.multiple_of(mp * 512, 512), 512)
    state = tokens[:, mine_cols].astype(F32) + msend[mp].astype(F32)
    wait_in(mrecv, M)
    for k in range(7):
        state = state + mrecv[k].astype(F32)
    u = (state * final_gain[:, mine_cols]).astype(BF16)
    xa[c, dp, y] = u[:, 0:256]
    xb[c, y, dp] = u[:, 256:512]
    for dev in y_peers:
        send(xa.at[c, dp, y], xa.at[c, dp, y], A1, dev)
    sent(xa.at[0, 0, pl.ds(0, 3)], A1)
    for dev in dp_peers:
        send(xb.at[c, y, dp], xb.at[c, y, dp], B1, dev)
    sent(xb.at[0, 0, pl.ds(0, 15)], B1)
    part = to_row(jnp.sum(state * state, axis=1, keepdims=True), 128)
    sqs[...] = jnp.broadcast_to(part, (8, 128))
    for k, dev in enumerate(mp_peers):
        send(sqs, sq1.at[k], Q1, dev)
    sent(sq1, Q1)
    wait_in(xa.at[0, 0, pl.ds(0, 3)], A1)
    for dev in dp_peers:
        send(xa.at[c, dp], xa.at[c, dp], A2, dev)
    sent(xa.at[0, pl.ds(0, 15)], A2)
    wait_in(sq1, Q1)
    total = sqs[...]
    for k in range(7):
        total = total + sq1[k]
    sq2[dp] = total
    for dev in dp_peers:
        send(sq2.at[dp], sq2.at[dp], Q2, dev)
    sent(sq2.at[pl.ds(0, 15)], Q2)
    wait_in(xb.at[0, 0, pl.ds(0, 15)], B1)
    for dev in y_peers:
        send(xb.at[c, y], xb.at[c, y], B2, dev)
    sent(xb.at[0, pl.ds(0, 3)], B2)
    need(temp, bhead)
    temp_col = to_col(temp[...], 256)
    wait_in(sq2.at[pl.ds(0, 15)], Q2)
    sums = sq2[:, 0:1, :]
    sums = jnp.sum(
        jnp.where((iota((16, 16, 128), 1) == iota((16, 16, 128), 2)), sums, 0.0),
        axis=2, keepdims=True,
    ).reshape(256, 1)
    row_scale = lax.rsqrt(sums * (1.0 / 4096.0) + EPS)

    wait_in(xa.at[0, pl.ds(0, 15)], A2)
    send(xa.at[c], xa.at[c], A3, sibling)
    sent(xa.at[0], A3)

    def head_a(cc, acc):
        for yy in range(4):
            rows = pl.ds(pl.multiple_of((2 * yy + cc) * 512, 256), 256)
            part = mm(xa[cc, :, yy].reshape(256, 256), bhead[rows, :])
            acc = part if acc is None else acc + part
        return acc

    def head_b(cc, acc):
        for yy in range(4):
            rows = pl.ds(pl.multiple_of((2 * yy + cc) * 512 + 256, 256), 256)
            acc = acc + mm(xb[cc, yy].reshape(256, 256), bhead[rows, :])
        return acc

    acc = head_a(c, None)
    wait_in(xb.at[0, pl.ds(0, 3)], B2)
    send(xb.at[c], xb.at[c], B3, sibling)
    sent(xb.at[0], B3)
    acc = head_b(c, acc)
    wait_in(xa.at[0], A3)
    acc = head_a(1 - c, acc)
    wait_in(xb.at[0], B3)
    acc = head_b(1 - c, acc)

    combined = temp_col * (acc * row_scale + slog[...])
    peak = jnp.max(combined, axis=1, keepdims=True)
    total = jnp.sum(jnp.exp(combined - peak), axis=1, keepdims=True)
    lsend[0, 0:1] = to_row(peak, 256)
    lsend[0, 1:2] = to_row(total, 256)

    def merge(pk, tt, buf, count):
        top = pk
        for k in range(count):
            top = jnp.maximum(top, buf[k, 0:1])
        out = tt * jnp.exp(pk - top)
        for k in range(count):
            out = out + buf[k, 1:2] * jnp.exp(buf[k, 0:1] - top)
        return top, out

    for k, dev in enumerate(dp_peers):
        send(lsend.at[0], l1.at[k], L1, dev)
    sent(l1, L1)
    wait_in(l1, L1)
    pk, tt = merge(lsend[0, 0:1], lsend[0, 1:2], l1, 15)
    lsend[1, 0:1] = pk
    lsend[1, 1:2] = tt
    for k, dev in enumerate(mp_peers):
        send(lsend.at[1], l2.at[k], L2, dev)
    sent(l2, L2)
    wait_in(l2, L2)
    pk, tt = merge(pk, tt, l2, 7)
    out_ref[...] = combined - to_col(pk, 256) - to_col(jnp.log(tt), 256)

    for ref, phase in pending:
        rcopy(ref, ref, phase, sibling).wait_send()


def per_device(
    tokens, norm_gain, router, w_gate, w_up, w_down, final_gain, routes, steer_hidden,
    steer_query, steer_cache, steer_new, cache_len, steer_out, steer_gain, base_head,
    steer_head, inv_temp,
):
    args = (
        tokens, norm_gain.reshape(1, -1), router.T, w_gate, w_up, w_down,
        final_gain.reshape(1, -1), routes.T, steer_hidden, steer_query, steer_cache, steer_new,
        cache_len.reshape(1, -1), steer_out, steer_gain, base_head, steer_head,
        inv_temp.reshape(1, -1),
    )
    d = tokens.shape[1]
    vs = base_head.shape[1]

    def like(a, drop=0):
        return pltpu.VMEM(a.shape[drop:], a.dtype)

    fetched = [like(a, 1 if k in (3, 4, 5) else 0) for k, a in enumerate(args)]
    scratch = fetched + [
        pltpu.VMEM((8, d), BF16),
        pltpu.VMEM((16, 8, d), BF16),
        pltpu.VMEM((128, w_gate.shape[2]), BF16),
        pltpu.VMEM((8, 2, 16, 128), F32),
        pltpu.VMEM((7, 2, 16, 128), F32),
        pltpu.VMEM((8, 2, 16, 128), F32),
        pltpu.VMEM((2, 4, 16, 16, 256), BF16),
        pltpu.VMEM((NC, 16, 8, d // NC), BF16),
        pltpu.VMEM((NC, 16, 8, d // NC), BF16),
        pltpu.VMEM((8, 16, 512), BF16),
        pltpu.VMEM((7, 16, 512), BF16),
        pltpu.VMEM((2, 16, 4, 16, 256), BF16),
        pltpu.VMEM((2, 4, 16, 16, 256), BF16),
        pltpu.VMEM((7, 8, 128), F32),
        pltpu.VMEM((16, 8, 128), F32),
        pltpu.VMEM((8, 128), F32),
        pltpu.VMEM((2, 2, 256), F32),
        pltpu.VMEM((15, 2, 256), F32),
        pltpu.VMEM((7, 2, 256), F32),
        pltpu.VMEM((256, vs), F32),
        pltpu.VMEM((16, 128), F32),
        pltpu.SemaphoreType.DMA((13 + 2 * WC + 3,)),
        pltpu.SemaphoreType.DMA((17 + NC,)),
        pltpu.SemaphoreType.DMA((17 + NC,)),
    ]
    return pl.pallas_call(
        kernel,
        name="decode_step",
        out_shape=jax.ShapeDtypeStruct((256, vs), F32),
        in_specs=[pl.BlockSpec(memory_space=pl.ANY)] * len(args),
        out_specs=pl.BlockSpec(memory_space=pltpu.VMEM),
        scratch_shapes=scratch,
        compiler_params=pltpu.CompilerParams(
            collective_id=0, has_side_effects=True, vmem_limit_bytes=60 * 1024 * 1024
        ),
    )(*args)


def solution(mesh):
    placed = (
        P("dp", None),
        P(),
        P(),
        P("mp", None, "dp"),
        P("mp", None, "dp"),
        P("mp", "dp", None),
        P(),
        P(),
        P(None, "dp", None),
        P(None, "dp", "mp"),
        P(None, None, "dp", None, "mp"),
        P(None, None, "dp", "mp"),
        P("dp"),
        P(None, "mp", None),
        P(),
        P(None, ("dp", "mp")),
        P(None, None, ("dp", "mp")),
        P(),
    )
    return jax.shard_map(
        per_device, mesh=mesh, in_specs=placed, out_specs=P(None, ("dp", "mp")), check_vma=False
    )
```

time: 208 us -> 74.2 us (0.36)
  waiting for transfers between devices: 95.2 us -> 0 us
  Pallas kernels: 0 us -> 70.4 us
  blocking collectives: 34.8 us -> 0 us
  starting transfers between devices: 24.8 us -> 0 us
  matrix products: 22.5 us -> 0 us
  between operations: 13.7 us -> 0.01 us
  local copies, waits for them, and re-layouts: 9.92 us -> 3.63 us
  other arithmetic: 5.86 us -> 0 us
    pallas_call x0 -> x1, Pallas kernels: none -> 70.4 us  [per_device(): pl.pallas_call(kernel, name='decode_step', out_shape=jax.ShapeDtypeStruct...]
    all_to_all x4 -> x0, waiting for transfers between devices: 55.4 us -> none  [the longest x3 42.1 us: copy_for_each(): lax.all_to_all(jnp.broadcast_to(x[None], (size, *x.shape)), axis, 0, 0, t...]
    all_gather x1 -> x0, waiting for transfers between devices: 39.7 us -> none  [rows_first(): filled, at, outs = (lax.all_gather(both, axis, axis=0, tiled=True), 0, [])]
    all_gather x4 -> x0, blocking collectives: 34.8 us -> none  [collected_together(): both, at, found = (lax.all_gather(jnp.concatenate(lines), axis), 0, {})]
    all_to_all x4 -> x0, starting transfers between devices: 24.8 us -> none  [the longest x3 20.5 us: copy_for_each(): lax.all_to_all(jnp.broadcast_to(x[None], (size, *x.shape)), axis, 0, 0, t...]
    dot_general x11 -> x0, matrix products: 22.5 us -> none  [the longest x1 8.64 us: per_device(): jnp.dot(hidden, down_mat, preferred_element_type=jnp.float32)]
    slice x3 -> x0, local copies, waits for them, and re-layouts: 3.38 us -> none  [the longest x1 2.08 us: per_device(): steer_head[1]]
    broadcast_in_dim x3 -> x0, local copies, waits for them, and re-layouts: 3.3 us -> none  [copy_for_each(): jnp.broadcast_to(x[None], (size, *x.shape))]
  transfers between devices with their start and end apart: 5 -> 0, of which waited for: 5 -> 0; matrix products, arithmetic and copies ran while one was open for 5% -> 0% of each run, Pallas kernels for 0% -> 0%
where the time goes in v1:
time: 74.2 us; the launch traced here: 74.1 us
  Pallas kernels  70.4 us (95%)
  local copies, waits for them, and re-layouts  3.63 us (5%)
    pallas_call x1, Pallas kernels, per_device(): pl.pallas_call(kernel, name='decode_step', out_shape=jax.ShapeDtypeStruct...  70.4 us
    unnamed x2, local copies, waits for them, and re-layouts  3.63 us

profile of v1, /device:TPU:1, one launch (start us, length us, event | category | flops | bytes accessed | tf_op | source)
XLA Modules:
  0.0 74.1 jit_solution(7742973275435100028)
XLA Ops:
  0.0 2.1 %copy.19.shead_h = bf16[2,1024,125]{2,1,0:T(8,128)(2,1)} copy(bf16[2,1024,125]{1,0,2:T(2,128)(2,1)} %param.34) | data formatting | bytes 1024000 | tf_op args[16]
  2.1 70.4 %decode_step.1 = f32[256,125]{1,0:T(8,128)} custom-call(bf16[16,4096]{1,0:T(8,128)(2,1)} %tokens_h.1, f32[1,4096]{1,0:T(1,128)} %bitcast.7, bf16[8,4096]{1,0:T(8,128)(2,1)} %bitcast.6, bf16[1,4096,896]{2,1,0:T(8,128)(2,1)} %w_gate_h.1, bf16[1,4096,896]{2,1,0:T(8,128)(2,1)} %w_up_h.1, bf16[1,896,4096]{2,1,0:T(8,128)(2,1)} %w_down_h.1, f32[1,4096]{1,0:T(1,128)} %bitcast.8, ...), custom_call_target="tpu_custom_call" | custom-call | tf_op jit(solution)/shard_map/decode_step/pallas_call | solution.py:450
  72.5 1.6 %copy.21 = f32[256,125]{1,0:T(8,128)} copy(f32[256,125]{1,0:T(8,128)} %decode_step.1) | data formatting | bytes 256000

commit v2 on v1

--- a/solution.py
+++ b/solution.py
@@ -13,7 +13,6 @@
 EPS = 1e-5
 ALPHA = 2.0
 HEAD_DIM = 128
-NC = 4
 WC = 4
 
 
@@ -49,8 +48,8 @@
     out_ref,
     tokens, norm_gain, router, w_gate, w_up, w_down, final_gain, routes,
     hidden, query, cache, new, clen, sout, sgain, bhead, shead, temp,
-    xs, xr, act, pbuf, prec, stbuf, sall, rsend, rrecv, msend, mrecv,
-    xa, xb, sq1, sq2, sqs, lsend, l1, l2, slog, comb_s,
+    xr, act, pbuf, prec, stbuf, sall, rsend, rrecv,
+    xa, xb, sq1, sq2, sqs, lsend, l1, l2, slog, combs,
     lsem, bsem_s, bsem_r,
 ):
     dp = lax.axis_index("dp")
@@ -58,14 +57,15 @@
     y, c = mp // 2, mp % 2
     z, x = dp // 4, dp % 4
 
+    zs = [z] + [lax.rem(z + k, 4) for k in (1, 2, 3)]
+    xs = [x] + [lax.rem(x + k, 4) for k in (1, 2, 3)]
+
+    def dp_at(kz, kx):
+        return zs[kz % 4] * 4 + xs[kx % 4]
+
     dp_peers = [
-        (lax.rem(z + k // 4, 4) * 4 + lax.rem(x + k % 4, 4), mp)
-        for k in (1, 3, 4, 12, 5, 7, 13, 15, 2, 8, 6, 14, 9, 11, 10)
+        (dp_at(k // 4, k % 4), mp) for k in (1, 3, 4, 12, 5, 7, 13, 15, 2, 8, 6, 14, 9, 11, 10)
     ]
-    dp_slot = (1, 3, 4, 12, 5, 7, 13, 15, 2, 8, 6, 14, 9, 11, 10)
-    def dp_from(k):
-        return (lax.rem(z + 4 - k // 4, 4) * 4 + lax.rem(x + 4 - k % 4, 4), mp)
-
     mp_peers = [(dp, lax.rem(mp + k, 8)) for k in range(1, 8)]
     y_peers = [(dp, lax.rem(y + k, 4) * 2 + c) for k in (1, 3, 2)]
     sibling = (dp, y * 2 + 1 - c)
@@ -82,13 +82,15 @@
         rcopy(src, dst, phase, dev).start()
 
     def wait_in(ref, phase):
-        rcopy(ref, ref, phase, sibling).wait_recv()
+        with jax.named_scope("wait%d" % phase):
+            rcopy(ref, ref, phase, sibling).wait_recv()
 
     def sent(ref, phase):
         pending.append((ref, phase))
 
-    (X, PR, ST, S1, S2, S3, M, A1, A2, A3, B1, B2, B3, Q1, Q2, L1, L2) = range(17)
-    R0 = 17
+    (XA, XB, PR, ST, S1, S2, S3, A1, A2, A3, B1, B2, B3, Q1, Q2, L1, L2) = range(17)
+    X1 = 16
+    R0 = 23
 
     pairs = [
         (tokens_h, tokens), (norm_gain_h, norm_gain), (routes_h, routes), (router_h, router),
@@ -123,8 +125,9 @@
         n += 1
 
     def need(*refs):
-        for r in refs:
-            copies[id(r)].wait()
+        with jax.named_scope("need"):
+            for r in refs:
+                copies[id(r)].wait()
 
     need(tokens, norm_gain, routes)
     tok = tokens[...].astype(F32)
@@ -135,11 +138,14 @@
     own = lanes == dp * 16 + iota((16, 256), 0)
     earlier = (lanes >= dp * 16) & (lanes < dp * 16 + iota((16, 256), 0))
     rt0, rt1 = rt[0:1, :], rt[1:2, :]
-    hit_all = ((rt0 == mp) | (rt1 == mp)).astype(F32)
-    r0 = jnp.sum(jnp.where(own, rt0.astype(F32), 0.0), axis=1, keepdims=True)
-    r1 = jnp.sum(jnp.where(own, rt1.astype(F32), 0.0), axis=1, keepdims=True)
-    hit = jnp.sum(jnp.where(own, hit_all, 0.0), axis=1, keepdims=True)
-    rank = jnp.sum(jnp.where(earlier, hit_all, 0.0), axis=1, keepdims=True)
+
+    def places(expert):
+        hit_all = ((rt0 == expert) | (rt1 == expert)).astype(F32)
+        hit = jnp.sum(jnp.where(own, hit_all, 0.0), axis=1, keepdims=True)
+        rank = jnp.sum(jnp.where(earlier, hit_all, 0.0), axis=1, keepdims=True)
+        return hit, rank
+
+    hit, _ = places(mp)
     hit_row = jnp.sum(jnp.where(eye(16, 128), hit, 0.0), axis=0, keepdims=True)
     rank_row = jnp.sum(
         jnp.where(iota((16, 128), 0) < iota((16, 128), 1), hit, 0.0), axis=0, keepdims=True
@@ -147,14 +153,38 @@
     select = jnp.where(
         (hit_row > 0.5) & (rank_row == iota((8, 128), 0).astype(F32)), 1.0, 0.0
     )[:, :16].astype(BF16)
-    slot_in = mm(select, normed).astype(BF16)
-    xs[...] = slot_in
-    xr[0] = slot_in
-
-    pl.semaphore_wait(barrier, 22)
-    for k, dev in zip(dp_slot, dp_peers):
-        send(xs, xr.at[k], X, dev)
-    sent(xr.at[pl.ds(0, 15)], X)
+    half = xr.shape[3]
+    xr[0, 0] = mm(select, normed[:, :half]).astype(BF16)
+    xr[1, 0] = mm(select, normed[:, half:]).astype(BF16)
+
+    with jax.named_scope("barrier"):
+        pl.semaphore_wait(barrier, 22)
+
+    def to_x(kx):
+        return (dp_at(0, kx), mp)
+
+    def to_z(kz):
+        return (dp_at(kz, 0), mp)
+
+    for k in (1, 3, 2):
+        send(xr.at[0, 0], xr.at[0, k], X1 + k, to_x(k))
+        send(xr.at[1, 0], xr.at[1, 4 * k], X1 + 3 + k, to_z(k))
+    for k in (1, 3, 2):
+        send(xr.at[0, 0], xr.at[0, 4 * k], XA, to_z(k))
+        send(xr.at[1, 0], xr.at[1, k], XB, to_x(k))
+
+    def forward(k):
+        wait_in(xr.at[0, k], X1 + k)
+        for kz in (1, 3, 2):
+            send(xr.at[0, k], xr.at[0, 4 * kz + k], XA, to_z(kz))
+        wait_in(xr.at[1, 4 * k], X1 + 3 + k)
+        for kx in (1, 3, 2):
+            send(xr.at[1, 4 * k], xr.at[1, 4 * k + kx], XB, to_x(kx))
+        sent(xr.at[0, 0], X1 + k)
+        sent(xr.at[0, 0], X1 + 3 + k)
+
+    sent(xr.at[0, pl.ds(0, 12)], XA)
+    sent(xr.at[1, pl.ds(0, 12)], XB)
 
     need(query, cache, new, clen, sout)
     len_col = to_col(clen[...].astype(F32), 16).astype(jnp.int32)
@@ -182,20 +212,24 @@
         send(pbuf.at[dev[1]], prec.at[k], PR, dev)
     sent(prec, PR)
 
+    for k in (1, 3, 2):
+        forward(k)
+
     need(router)
     logits = nt(normed, router[...])
     experts = iota((16, 8), 1).astype(F32)
+    r0 = jnp.sum(jnp.where(own, rt0.astype(F32), 0.0), axis=1, keepdims=True)
+    r1 = jnp.sum(jnp.where(own, rt1.astype(F32), 0.0), axis=1, keepdims=True)
     p0 = jnp.sum(jnp.where(experts == r0, logits, 0.0), axis=1, keepdims=True)
     p1 = jnp.sum(jnp.where(experts == r1, logits, 0.0), axis=1, keepdims=True)
-    mine = mp.astype(F32)
-    gate = jnp.where(
-        r0 == mine,
-        1.0 / (1.0 + jnp.exp(p1 - p0)),
-        jnp.where(r1 == mine, 1.0 / (1.0 + jnp.exp(p0 - p1)), 0.0),
-    )
-    comb_s[...] = jnp.where(
-        (hit > 0.5) & (rank == iota((16, 128), 1).astype(F32)), gate, 0.0
-    )
+    gate0 = 1.0 / (1.0 + jnp.exp(p1 - p0))
+    gate1 = 1.0 / (1.0 + jnp.exp(p0 - p1))
+    for i in range(8):
+        expert = lax.rem(mp + 8 - i, 8)
+        named = expert.astype(F32)
+        _, rank = places(expert)
+        gate = jnp.where(r0 == named, gate0, 0.0) + jnp.where(r1 == named, gate1, 0.0)
+        combs[i] = jnp.where(rank == iota((16, 128), 1).astype(F32), gate, 0.0)
 
     need(hidden, sgain)
     wait_in(prec, PR)
@@ -213,24 +247,26 @@
         part = stbuf[e, c]
         sq_sum = sq_sum + jnp.sum(part * part, axis=1, keepdims=True)
     inv = lax.rsqrt(sq_sum * (1.0 / 1024.0) + EPS)
-    for h in range(2):
-        cols = pl.ds(pl.multiple_of(y * 256 + h * 128, 128), 128)
-        both = sgain[:, cols]
-        g = jnp.where(c == 0, both[0:1], both[1:2])
-        sall[c, y, dp, :, h * 128 : (h + 1) * 128] = (stbuf[2 * y + h, c] * inv * g).astype(BF16)
+    both = sgain[...]
+    g = jnp.where(c == 0, both[0:1], both[1:2])
+    for e in range(8):
+        cols = slice(e * 128, (e + 1) * 128)
+        sall[c, dp, :, cols] = (stbuf[e, c] * inv * g[:, cols]).astype(BF16)
     for dev in dp_peers:
-        send(sall.at[c, y, dp], sall.at[c, y, dp], S1, dev)
-    sent(sall.at[0, 0, pl.ds(0, 15)], S1)
-
-    wait_in(xr.at[pl.ds(1, 15)], X)
-    for cp in wcopies:
-        cp.wait()
-    kx = xr.shape[2]
+        send(sall.at[c, dp], sall.at[c, dp], S1, dev)
+    sent(sall.at[0, pl.ds(0, 15)], S1)
+
+    wait_in(xr.at[0, pl.ds(0, 12)], XA)
+    wait_in(xr.at[1, pl.ds(0, 12)], XB)
+    with jax.named_scope("weights"):
+        for cp in wcopies:
+            cp.wait()
 
     def up_tile(col, width):
-        rows = xr[...].reshape(128, kx)
-        g = mm(rows, w_gate[:, pl.ds(col, width)])
-        u = mm(rows, w_up[:, pl.ds(col, width)])
+        cols = pl.ds(col, width)
+        lo, hi = xr[0].reshape(128, half), xr[1].reshape(128, half)
+        g = mm(lo, w_gate[:half, cols]) + mm(hi, w_gate[half:, cols])
+        u = mm(lo, w_up[:half, cols]) + mm(hi, w_up[half:, cols])
         act[:, pl.ds(col, width)] = (g / (1.0 + jnp.exp(-g)) * u).astype(BF16)
 
     ff = w_gate.shape[1]
@@ -244,65 +280,46 @@
     if ff % 256:
         up_tile(full * 256, ff % 256)
 
-    wait_in(sall.at[0, 0, pl.ds(0, 15)], S1)
-    for dev in y_peers:
-        send(sall.at[c, y], sall.at[c, y], S2, dev)
-    sent(sall.at[0, pl.ds(0, 3)], S2)
-
     need(w_down)
-    wn = w_down.shape[1] // NC
-    for q in range(NC):
-        def down_body(i, carry):
-            col = pl.multiple_of(q * wn + i * 256, 256)
+    wn = rsend.shape[3]
+    for i in range(8):
+        owner = lax.rem(mp + i, 8)
+        for h in range(wn // 256):
+            col = pl.multiple_of(owner * wn + h * 256, 256)
             res = mm(act[...], w_down[:, pl.ds(col, 256)])
-            rsend[q, :, :, pl.ds(pl.multiple_of(i * 256, 256), 256)] = res.reshape(
-                16, 8, 256
-            ).astype(BF16)
-            return carry
-
-        lax.fori_loop(0, wn // 256, down_body, 0)
-        for k in dp_slot:
-            send(rsend.at[q, k], rrecv.at[q, k], R0 + q, dp_from(k))
-        sent(rsend.at[q, pl.ds(0, 15)], R0 + q)
-
-    wait_in(sall.at[0, pl.ds(0, 3)], S2)
+            rsend[i, :, :, h * 256 : (h + 1) * 256] = res.reshape(16, 8, 256).astype(BF16)
+        for k in range(0 if i else 1, 16):
+            send(
+                rsend.at[i, k], rrecv.at[i, k], R0 + i,
+                (dp_at(4 - k // 4, 4 - k % 4), owner),
+            )
+        sent(rsend.at[i, pl.ds(0, 16 if i else 15)], R0 + i)
+
+    wait_in(sall.at[0, pl.ds(0, 15)], S1)
     send(sall.at[c], sall.at[c], S3, sibling)
     sent(sall.at[0], S3)
     need(shead)
     wait_in(sall.at[0], S3)
-    for m in range(2):
-        acc = None
-        for yy in range(4):
-            part = mm(sall[m, yy].reshape(256, 256), shead[m, yy * 256 : (yy + 1) * 256, :])
-            acc = part if acc is None else acc + part
-        if m == 0:
-            slog[...] = acc
+    slog[...] = ALPHA * (
+        nt(sall[0].reshape(256, 1024), shead[:, 0, :])
+        - nt(sall[1].reshape(256, 1024), shead[:, 1, :])
+    )
+
+    need(final_gain)
+    mine_cols = pl.ds(pl.multiple_of(mp * wn, wn), wn)
+    state = tokens[:, mine_cols].astype(F32)
+    for i in range(8):
+        if i:
+            wait_in(rrecv.at[i], R0 + i)
+            total = rrecv[i, 0].astype(F32)
         else:
-            slog[...] = ALPHA * (slog[...] - acc)
-
-    comb = comb_s[...]
-    for q in range(NC):
-        wait_in(rrecv.at[q, pl.ds(1, 15)], R0 + q)
-        total = rsend[q, 0].astype(F32)
+            wait_in(rrecv.at[i, pl.ds(1, 15)], R0 + i)
+            total = rsend[i, 0].astype(F32)
         for k in range(1, 16):
-            total = total + rrecv[q, k].astype(F32)
-        mixed = None
+            total = total + rrecv[i, k].astype(F32)
+        comb = combs[i]
         for s in range(8):
-            term = comb[:, s : s + 1] * total[s : s + 1, :]
-            mixed = term if mixed is None else mixed + term
-        mixed = mixed.astype(BF16)
-        per = wn // 512
-        for h in range(per):
-            msend[q * per + h] = mixed[:, h * 512 : (h + 1) * 512]
-    for k, dev in enumerate(mp_peers):
-        send(msend.at[dev[1]], mrecv.at[k], M, dev)
-    sent(mrecv, M)
-    need(final_gain)
-    mine_cols = pl.ds(pl.multiple_of(mp * 512, 512), 512)
-    state = tokens[:, mine_cols].astype(F32) + msend[mp].astype(F32)
-    wait_in(mrecv, M)
-    for k in range(7):
-        state = state + mrecv[k].astype(F32)
+            state = state + comb[:, s : s + 1] * total[s : s + 1, :]
     u = (state * final_gain[:, mine_cols]).astype(BF16)
     xa[c, dp, y] = u[:, 0:256]
     xb[c, y, dp] = u[:, 256:512]
@@ -335,6 +352,9 @@
     sent(xb.at[0, pl.ds(0, 3)], B2)
     need(temp, bhead)
     temp_col = to_col(temp[...], 256)
+    wait_in(xa.at[0, pl.ds(0, 15)], A2)
+    send(xa.at[c], xa.at[c], A3, sibling)
+    sent(xa.at[0], A3)
     wait_in(sq2.at[pl.ds(0, 15)], Q2)
     sums = sq2[:, 0:1, :]
     sums = jnp.sum(
@@ -343,9 +363,6 @@
     ).reshape(256, 1)
     row_scale = lax.rsqrt(sums * (1.0 / 4096.0) + EPS)
 
-    wait_in(xa.at[0, pl.ds(0, 15)], A2)
-    send(xa.at[c], xa.at[c], A3, sibling)
-    sent(xa.at[0], A3)
 
     def head_a(cc, acc):
         for yy in range(4):
@@ -372,32 +389,30 @@
 
     combined = temp_col * (acc * row_scale + slog[...])
     peak = jnp.max(combined, axis=1, keepdims=True)
-    total = jnp.sum(jnp.exp(combined - peak), axis=1, keepdims=True)
-    lsend[0, 0:1] = to_row(peak, 256)
-    lsend[0, 1:2] = to_row(total, 256)
-
-    def merge(pk, tt, buf, count):
-        top = pk
+    lse = peak + jnp.log(jnp.sum(jnp.exp(combined - peak), axis=1, keepdims=True))
+
+    def merge(first, buf, count):
+        top = first
         for k in range(count):
-            top = jnp.maximum(top, buf[k, 0:1])
-        out = tt * jnp.exp(pk - top)
+            top = jnp.maximum(top, buf[k])
+        out = jnp.exp(first - top)
         for k in range(count):
-            out = out + buf[k, 1:2] * jnp.exp(buf[k, 0:1] - top)
-        return top, out
-
+            out = out + jnp.exp(buf[k] - top)
+        return top + jnp.log(out)
+
+    row = to_row(lse, 256)
+    lsend[0] = row
     for k, dev in enumerate(dp_peers):
         send(lsend.at[0], l1.at[k], L1, dev)
     sent(l1, L1)
     wait_in(l1, L1)
-    pk, tt = merge(lsend[0, 0:1], lsend[0, 1:2], l1, 15)
-    lsend[1, 0:1] = pk
-    lsend[1, 1:2] = tt
+    row = merge(row, l1, 15)
+    lsend[1] = row
     for k, dev in enumerate(mp_peers):
         send(lsend.at[1], l2.at[k], L2, dev)
     sent(l2, L2)
     wait_in(l2, L2)
-    pk, tt = merge(pk, tt, l2, 7)
-    out_ref[...] = combined - to_col(pk, 256) - to_col(jnp.log(tt), 256)
+    out_ref[...] = combined - to_col(merge(row, l2, 7), 256)
 
     for ref, phase in pending:
         rcopy(ref, ref, phase, sibling).wait_send()
@@ -411,8 +426,8 @@
     args = (
         tokens, norm_gain.reshape(1, -1), router.T, w_gate, w_up, w_down,
         final_gain.reshape(1, -1), routes.T, steer_hidden, steer_query, steer_cache, steer_new,
-        cache_len.reshape(1, -1), steer_out, steer_gain, base_head, steer_head,
-        inv_temp.reshape(1, -1),
+        cache_len.reshape(1, -1), steer_out, steer_gain, base_head,
+        jnp.transpose(steer_head, (2, 0, 1)), inv_temp.reshape(1, -1),
     )
     d = tokens.shape[1]
     vs = base_head.shape[1]
@@ -422,42 +437,39 @@
 
     fetched = [like(a, 1 if k in (3, 4, 5) else 0) for k, a in enumerate(args)]
     scratch = fetched + [
-        pltpu.VMEM((8, d), BF16),
-        pltpu.VMEM((16, 8, d), BF16),
+        pltpu.VMEM((2, 16, 8, d // 2), BF16),
         pltpu.VMEM((128, w_gate.shape[2]), BF16),
         pltpu.VMEM((8, 2, 16, 128), F32),
         pltpu.VMEM((7, 2, 16, 128), F32),
         pltpu.VMEM((8, 2, 16, 128), F32),
-        pltpu.VMEM((2, 4, 16, 16, 256), BF16),
-        pltpu.VMEM((NC, 16, 8, d // NC), BF16),
-        pltpu.VMEM((NC, 16, 8, d // NC), BF16),
-        pltpu.VMEM((8, 16, 512), BF16),
-        pltpu.VMEM((7, 16, 512), BF16),
+        pltpu.VMEM((2, 16, 16, 1024), BF16),
+        pltpu.VMEM((8, 16, 8, d // 8), BF16),
+        pltpu.VMEM((8, 16, 8, d // 8), BF16),
         pltpu.VMEM((2, 16, 4, 16, 256), BF16),
         pltpu.VMEM((2, 4, 16, 16, 256), BF16),
         pltpu.VMEM((7, 8, 128), F32),
         pltpu.VMEM((16, 8, 128), F32),
         pltpu.VMEM((8, 128), F32),
-        pltpu.VMEM((2, 2, 256), F32),
-        pltpu.VMEM((15, 2, 256), F32),
-        pltpu.VMEM((7, 2, 256), F32),
+        pltpu.VMEM((2, 1, 256), F32),
+        pltpu.VMEM((15, 1, 256), F32),
+        pltpu.VMEM((7, 1, 256), F32),
         pltpu.VMEM((256, vs), F32),
-        pltpu.VMEM((16, 128), F32),
+        pltpu.VMEM((8, 16, 128), F32),
         pltpu.SemaphoreType.DMA((13 + 2 * WC + 3,)),
-        pltpu.SemaphoreType.DMA((17 + NC,)),
-        pltpu.SemaphoreType.DMA((17 + NC,)),
+        pltpu.SemaphoreType.DMA((31,)),
+        pltpu.SemaphoreType.DMA((31,)),
     ]
     return pl.pallas_call(
         kernel,
         name="decode_step",
         out_shape=jax.ShapeDtypeStruct((256, vs), F32),
-        in_specs=[pl.BlockSpec(memory_space=pl.ANY)] * len(args),
+        in_specs=[pl.BlockSpec(memory_space=pltpu.HBM)] * len(args),
         out_specs=pl.BlockSpec(memory_space=pltpu.VMEM),
         scratch_shapes=scratch,
         compiler_params=pltpu.CompilerParams(
-            collective_id=0, has_side_effects=True, vmem_limit_bytes=60 * 1024 * 1024
+            collective_id=0, has_side_effects=True, vmem_limit_bytes=44 * 1024 * 1024
         ),
-    )(*args)
+    )(*[pltpu.with_memory_space_constraint(a, pltpu.HBM) for a in args])
 
 
 def solution(mesh):

time: 74.2 us -> 63.8 us (0.86)
  Pallas kernels: 70.4 us -> 63 us
  local copies, waits for them, and re-layouts: 3.63 us -> 0.66 us
    pallas_call x1, Pallas kernels: 70.4 us -> 63 us  [per_device(): pl.pallas_call(kernel, name='decode_step', out_shape=jax.ShapeDtypeStruct...]
    unnamed x2 -> x1, local copies, waits for them, and re-layouts: 3.63 us -> 0.66 us
where the time goes in v2:
time: 63.8 us; the launch traced here: 63.7 us
  Pallas kernels  63 us (99%)
  local copies, waits for them, and re-layouts  0.66 us (1%)
    pallas_call x1, Pallas kernels, per_device(): pl.pallas_call(kernel, name='decode_step', out_shape=jax.ShapeDtypeStruct...  63 us

profile of v2, /device:TPU:1, one launch (start us, length us, event | category | flops | bytes accessed | tf_op | source)
XLA Modules:
  0.0 63.7 jit_solution(7524766699310714758)
XLA Ops:
  0.0 63.0 %decode_step.1 = f32[256,125]{1,0:T(8,128)S(1)} custom-call(bf16[16,4096]{1,0:T(8,128)(2,1)} %tokens_h.1, f32[1,4096]{1,0:T(1,128)} %bitcast.9, bf16[8,4096]{1,0:T(8,128)(2,1)} %bitcast.8, bf16[1,4096,896]{2,1,0:T(8,128)(2,1)} %w_gate_h.1, bf16[1,4096,896]{2,1,0:T(8,128)(2,1)} %w_up_h.1, bf16[1,896,4096]{2,1,0:T(8,128)(2,1)} %w_down_h.1, ...), custom_call_target="tpu_custom_call" | custom-call | tf_op jit(solution)/shard_map/decode_step/pallas_call | solution.py:462
  63.0 0.7 %copy.20 = f32[256,125]{1,0:T(8,128)} copy(f32[256,125]{1,0:T(8,128)S(1)} %decode_step.1) | data formatting | bytes 256000

commit v3 on v2

--- a/solution.py
+++ b/solution.py
@@ -48,8 +48,8 @@
     out_ref,
     tokens, norm_gain, router, w_gate, w_up, w_down, final_gain, routes,
     hidden, query, cache, new, clen, sout, sgain, bhead, shead, temp,
-    xr, act, pbuf, prec, stbuf, sall, rsend, rrecv,
-    xa, xb, sq1, sq2, sqs, lsend, l1, l2, slog, combs,
+    xr, act, pbuf, prec, stbuf, sall, r1s, r1r, r2s, r2r, m1s, m1r, d2s, d2r, gs, gr, wh, wl,
+    xa, xb, bhs, psib, prcv, pown, sq1, sq2, sqs, lsend, l1, l2, slog, comb_s,
     lsem, bsem_s, bsem_r,
 ):
     dp = lax.axis_index("dp")
@@ -88,9 +88,8 @@
     def sent(ref, phase):
         pending.append((ref, phase))
 
-    (XA, XB, PR, ST, S1, S2, S3, A1, A2, A3, B1, B2, B3, Q1, Q2, L1, L2) = range(17)
-    X1 = 16
-    R0 = 23
+    (XA, XB, PR, ST, SA, SB, S3, A2, B1, B2, HD, PX, Q1, Q2, L1, L2, G, M1, D2, R2, R1) = range(21)
+    X1, Y1 = 21, 27
 
     pairs = [
         (tokens_h, tokens), (norm_gain_h, norm_gain), (routes_h, routes), (router_h, router),
@@ -145,7 +144,7 @@
         rank = jnp.sum(jnp.where(earlier, hit_all, 0.0), axis=1, keepdims=True)
         return hit, rank
 
-    hit, _ = places(mp)
+    hit, rank = places(mp)
     hit_row = jnp.sum(jnp.where(eye(16, 128), hit, 0.0), axis=0, keepdims=True)
     rank_row = jnp.sum(
         jnp.where(iota((16, 128), 0) < iota((16, 128), 1), hit, 0.0), axis=0, keepdims=True
@@ -156,35 +155,6 @@
     half = xr.shape[3]
     xr[0, 0] = mm(select, normed[:, :half]).astype(BF16)
     xr[1, 0] = mm(select, normed[:, half:]).astype(BF16)
-
-    with jax.named_scope("barrier"):
-        pl.semaphore_wait(barrier, 22)
-
-    def to_x(kx):
-        return (dp_at(0, kx), mp)
-
-    def to_z(kz):
-        return (dp_at(kz, 0), mp)
-
-    for k in (1, 3, 2):
-        send(xr.at[0, 0], xr.at[0, k], X1 + k, to_x(k))
-        send(xr.at[1, 0], xr.at[1, 4 * k], X1 + 3 + k, to_z(k))
-    for k in (1, 3, 2):
-        send(xr.at[0, 0], xr.at[0, 4 * k], XA, to_z(k))
-        send(xr.at[1, 0], xr.at[1, k], XB, to_x(k))
-
-    def forward(k):
-        wait_in(xr.at[0, k], X1 + k)
-        for kz in (1, 3, 2):
-            send(xr.at[0, k], xr.at[0, 4 * kz + k], XA, to_z(kz))
-        wait_in(xr.at[1, 4 * k], X1 + 3 + k)
-        for kx in (1, 3, 2):
-            send(xr.at[1, 4 * k], xr.at[1, 4 * k + kx], XB, to_x(kx))
-        sent(xr.at[0, 0], X1 + k)
-        sent(xr.at[0, 0], X1 + 3 + k)
-
-    sent(xr.at[0, pl.ds(0, 12)], XA)
-    sent(xr.at[1, pl.ds(0, 12)], XB)
 
     need(query, cache, new, clen, sout)
     len_col = to_col(clen[...].astype(F32), 16).astype(jnp.int32)
@@ -208,12 +178,49 @@
         proj = mm(att.astype(BF16), sout[m])
         for e in range(8):
             pbuf[e, m] = proj[:, e * 128 : (e + 1) * 128]
+    with jax.named_scope("barrier"):
+        pl.semaphore_wait(barrier, 22)
+
+    def to_x(kx):
+        return (dp_at(0, kx), mp)
+
+    def to_z(kz):
+        return (dp_at(kz, 0), mp)
+
+    def spread(buf, base, pa, pb):
+        for k in (1, 3, 2):
+            send(buf(0, 0, 0, 0), buf(0, 0, 0, k), base + k, to_x(k))
+            send(buf(1, 0, 0, 0), buf(1, 0, k, 0), base + 3 + k, to_z(k))
+        for k in (1, 3, 2):
+            send(buf(0, 0, 0, 0), buf(0, 0, k, 0), pa, to_z(k))
+            send(buf(1, 0, 0, 0), buf(1, 0, 0, k), pb, to_x(k))
+
+    def forward(buf, base, pa, pb):
+        for k in (1, 3, 2):
+            wait_in(buf(0, k, 0, 0), base + k)
+            for kz in (1, 3, 2):
+                send(buf(0, k, 0, 0), buf(0, k, kz, 0), pa, to_z(kz))
+            wait_in(buf(1, 4 * k, 0, 0), base + 3 + k)
+            for kx in (1, 3, 2):
+                send(buf(1, 4 * k, 0, 0), buf(1, 4 * k, 0, kx), pb, to_x(kx))
+            sent(buf(0, 0, 0, 0), base + k)
+            sent(buf(0, 0, 0, 0), base + 3 + k)
+
+    def xblock(colour, place, az, ax):
+        return xr.at[colour, place + 4 * az + ax]
+
+    def sblock(colour, place, az, ax):
+        return sall.at[c, colour, dp_at(4 - place // 4, 4 - place % 4)]
+
+    spread(xblock, X1, XA, XB)
+    sent(xr.at[0, pl.ds(0, 12)], XA)
+    sent(xr.at[1, pl.ds(0, 12)], XB)
+
     for k, dev in enumerate(mp_peers):
         send(pbuf.at[dev[1]], prec.at[k], PR, dev)
     sent(prec, PR)
 
-    for k in (1, 3, 2):
-        forward(k)
+    forward(xblock, X1, XA, XB)
 
     need(router)
     logits = nt(normed, router[...])
@@ -224,12 +231,15 @@
     p1 = jnp.sum(jnp.where(experts == r1, logits, 0.0), axis=1, keepdims=True)
     gate0 = 1.0 / (1.0 + jnp.exp(p1 - p0))
     gate1 = 1.0 / (1.0 + jnp.exp(p0 - p1))
-    for i in range(8):
-        expert = lax.rem(mp + 8 - i, 8)
-        named = expert.astype(F32)
-        _, rank = places(expert)
-        gate = jnp.where(r0 == named, gate0, 0.0) + jnp.where(r1 == named, gate1, 0.0)
-        combs[i] = jnp.where(rank == iota((16, 128), 1).astype(F32), gate, 0.0)
+    gs[0:1] = to_row(gate0, 128)
+    gs[1:2] = to_row(gate1, 128)
+    gr[dp] = gs[...]
+    for dev in dp_peers:
+        send(gs, gr.at[dp], G, dev)
+    sent(gr.at[pl.ds(0, 15)], G)
+    mine = mp.astype(F32)
+    gate = jnp.where(r0 == mine, gate0, 0.0) + jnp.where(r1 == mine, gate1, 0.0)
+    comb_s[...] = jnp.where(rank == iota((16, 128), 1).astype(F32), gate, 0.0)
 
     need(hidden, sgain)
     wait_in(prec, PR)
@@ -251,13 +261,19 @@
     g = jnp.where(c == 0, both[0:1], both[1:2])
     for e in range(8):
         cols = slice(e * 128, (e + 1) * 128)
-        sall[c, dp, :, cols] = (stbuf[e, c] * inv * g[:, cols]).astype(BF16)
-    for dev in dp_peers:
-        send(sall.at[c, dp], sall.at[c, dp], S1, dev)
-    sent(sall.at[0, pl.ds(0, 15)], S1)
+        inner = slice(e % 4 * 128, (e % 4 + 1) * 128)
+        sall[c, e // 4, dp, :, inner] = (stbuf[e, c] * inv * g[:, cols]).astype(BF16)
+    need(bhead)
+    for yy in range(4):
+        rows = pl.ds(pl.multiple_of((2 * yy + 1 - c) * 512, 512), 512)
+        send(bhead.at[rows], bhs.at[yy], HD, sibling)
+    sent(bhs, HD)
 
     wait_in(xr.at[0, pl.ds(0, 12)], XA)
     wait_in(xr.at[1, pl.ds(0, 12)], XB)
+    spread(sblock, Y1, SA, SB)
+    sent(sall.at[0, 0, pl.ds(0, 12)], SA)
+    sent(sall.at[0, 1, pl.ds(0, 12)], SB)
     with jax.named_scope("weights"):
         for cp in wcopies:
             cp.wait()
@@ -280,114 +296,178 @@
     if ff % 256:
         up_tile(full * 256, ff % 256)
 
+    forward(sblock, Y1, SA, SB)
     need(w_down)
-    wn = rsend.shape[3]
-    for i in range(8):
-        owner = lax.rem(mp + i, 8)
-        for h in range(wn // 256):
-            col = pl.multiple_of(owner * wn + h * 256, 256)
-            res = mm(act[...], w_down[:, pl.ds(col, 256)])
-            rsend[i, :, :, h * 256 : (h + 1) * 256] = res.reshape(16, 8, 256).astype(BF16)
-        for k in range(0 if i else 1, 16):
-            send(
-                rsend.at[i, k], rrecv.at[i, k], R0 + i,
-                (dp_at(4 - k // 4, 4 - k % 4), owner),
-            )
-        sent(rsend.at[i, pl.ds(0, 16 if i else 15)], R0 + i)
-
-    wait_in(sall.at[0, pl.ds(0, 15)], S1)
+    for core in range(2):
+        phase = R1 if core == 0 else Y1 + 7
+        for k in (2, 1, 3, 0):
+            to_y = lax.rem(y + k, 4)
+            owner = 2 * to_y + core
+            res = mm(act[...], w_down[:, pl.ds(pl.multiple_of(owner * 512, 512), 512)])
+            inner = pl.ds(pl.multiple_of(to_y * 256, 256), 256)
+            r1s[core, :, :, inner] = res[:, :256].reshape(16, 8, 256).astype(BF16)
+            second = res[:, 256:].astype(BF16)
+            r2s[core, k] = second
+            if k:
+                send(r2s.at[core, k], r2r.at[mp], R2, (dp, owner))
+            else:
+
+                @pl.when(c != core)
+                def _():
+                    send(r2s.at[core, 0], r2r.at[mp], R2, (dp, owner))
+
+                @pl.when(c == core)
+                def _():
+                    r2r[mp] = second
+
+        for k in (1, 3, 4, 12, 5, 7, 13, 15, 2, 8, 6, 14, 9, 11, 10):
+            send(r1s.at[core, k], r1r.at[core, k], phase, (dp_at(4 - k // 4, 4 - k % 4), mp))
+        sent(r1r.at[0, pl.ds(0, 15)], phase)
+    sent(r2r.at[pl.ds(0, 7)], R2)
+
+    wait_in(gr.at[pl.ds(0, 15)], G)
+
+    def spread_rows(rows):
+        diag = iota((16, 16, 128), 1) == iota((16, 16, 128), 2)
+        return jnp.sum(jnp.where(diag, rows, 0.0), axis=2, keepdims=True).reshape(256, 1)
+
+    route0, route1 = to_col(rt0.astype(F32), 256), to_col(rt1.astype(F32), 256)
+    lane = iota((256, 128), 1)
+    named0, named1 = lane.astype(F32) == route0, lane.astype(F32) == route1
+    t_row, t_col = iota((256, 256), 0), iota((256, 256), 1)
+    before = ((t_row >> 4) == (t_col >> 4)) & (t_col < t_row)
+    ranks = mm(
+        jnp.where(before, 1.0, 0.0).astype(BF16), jnp.where(named0 | named1, 1.0, 0.0).astype(BF16)
+    )
+    gates = jnp.where(named0, spread_rows(gr[:, 0:1, :]), 0.0) + jnp.where(
+        named1, spread_rows(gr[:, 1:2, :]), 0.0
+    )
+    block = ((z + 4 - (lane >> 5)) & 3) * 4 + ((x + 4 - ((lane >> 3) & 3)) & 3)
+    same = (iota((256, 128), 0) >> 4) == block
+    slot = (lane & 7).astype(F32)
+    for e in range(8):
+        w = jnp.where(same & (ranks[:, e : e + 1] == slot), gates[:, e : e + 1], 0.0)
+        high = w.astype(BF16)
+        wh[:, e * 128 : (e + 1) * 128] = high
+        wl[:, e * 128 : (e + 1) * 128] = (w - high.astype(F32)).astype(BF16)
+
+    wait_in(sall.at[0, 0, pl.ds(0, 12)], SA)
+    wait_in(sall.at[0, 1, pl.ds(0, 12)], SB)
     send(sall.at[c], sall.at[c], S3, sibling)
     sent(sall.at[0], S3)
     need(shead)
     wait_in(sall.at[0], S3)
-    slog[...] = ALPHA * (
-        nt(sall[0].reshape(256, 1024), shead[:, 0, :])
-        - nt(sall[1].reshape(256, 1024), shead[:, 1, :])
-    )
+    for m in range(2):
+        head = shead[:, m, :]
+        part = nt(sall[m, 0].reshape(256, 512), head[:, :512]) + nt(
+            sall[m, 1].reshape(256, 512), head[:, 512:]
+        )
+        slog[...] = part if m == 0 else ALPHA * (slog[...] - part)
 
     need(final_gain)
-    mine_cols = pl.ds(pl.multiple_of(mp * wn, wn), wn)
-    state = tokens[:, mine_cols].astype(F32)
-    for i in range(8):
-        if i:
-            wait_in(rrecv.at[i], R0 + i)
-            total = rrecv[i, 0].astype(F32)
-        else:
-            wait_in(rrecv.at[i, pl.ds(1, 15)], R0 + i)
-            total = rsend[i, 0].astype(F32)
+
+    def over_dp(buf, phase):
+        for dev in dp_peers:
+            send(buf, buf, phase, dev)
+
+    comb = comb_s[...]
+
+    def mix(core):
+        phase = R1 if core == 0 else Y1 + 7
+        wait_in(r1r.at[core, pl.ds(1, 15)], phase)
+        total = r1s[core, 0].astype(F32)
         for k in range(1, 16):
-            total = total + rrecv[i, k].astype(F32)
-        comb = combs[i]
-        for s in range(8):
-            state = state + comb[:, s : s + 1] * total[s : s + 1, :]
-    u = (state * final_gain[:, mine_cols]).astype(BF16)
-    xa[c, dp, y] = u[:, 0:256]
-    xb[c, y, dp] = u[:, 256:512]
-    for dev in y_peers:
-        send(xa.at[c, dp, y], xa.at[c, dp, y], A1, dev)
-    sent(xa.at[0, 0, pl.ds(0, 3)], A1)
-    for dev in dp_peers:
-        send(xb.at[c, y, dp], xb.at[c, y, dp], B1, dev)
-    sent(xb.at[0, 0, pl.ds(0, 15)], B1)
-    part = to_row(jnp.sum(state * state, axis=1, keepdims=True), 128)
-    sqs[...] = jnp.broadcast_to(part, (8, 128))
+            total = total + r1r[core, k].astype(F32)
+        mixed = comb[:, 0:1] * total[0:1, :]
+        for s in range(1, 8):
+            mixed = mixed + comb[:, s : s + 1] * total[s : s + 1, :]
+        m1s[core] = mixed.astype(BF16)
+        for k in range(4):
+            dev = (dp, 2 * lax.rem(y + k, 4) + core)
+            if k:
+                send(m1s.at[core], m1r.at[mp], M1, dev)
+            else:
+
+                @pl.when(c != core)
+                def _():
+                    send(m1s.at[core], m1r.at[mp], M1, dev)
+
+    mix(0)
+    wait_in(r2r.at[pl.ds(0, 7)], R2)
+    rows = r2r[...].reshape(1024, 256)
+    d2s[...] = (mm(wh[...], rows) + mm(wl[...], rows)).astype(BF16).reshape(16, 16, 256)
+    for k, dev in enumerate(dp_peers):
+        send(d2s.at[dev[0]], d2r.at[k], D2, dev)
+    sent(d2r, D2)
+    mix(1)
+    sent(m1r.at[pl.ds(0, 7)], M1)
+    m1r[mp] = m1s[c]
+
+    wait_in(d2r, D2)
+    cols = pl.ds(pl.multiple_of(mp * 512 + 256, 256), 256)
+    state = tokens[:, cols].astype(F32) + d2s[dp].astype(F32)
+    for k in range(15):
+        state = state + d2r[k].astype(F32)
+    xb[y, dp] = (state * final_gain[:, cols]).astype(BF16)
+    over_dp(xb.at[y, dp], B1)
+    sent(xb.at[0, pl.ds(0, 15)], B1)
+    square = jnp.sum(state * state, axis=1, keepdims=True)
+
+    wait_in(m1r.at[pl.ds(0, 7)], M1)
+    square1 = jnp.zeros((16, 1), F32)
+    for yy in range(4):
+        cols = pl.ds(pl.multiple_of((2 * yy + c) * 512, 256), 256)
+        inner = slice(yy * 256, (yy + 1) * 256)
+        state = tokens[:, cols].astype(F32)
+        for e in range(8):
+            state = state + m1r[e, :, inner].astype(F32)
+        xa[dp, :, inner] = (state * final_gain[:, cols]).astype(BF16)
+        square1 = square1 + jnp.sum(state * state, axis=1, keepdims=True)
+    over_dp(xa.at[dp], A2)
+    sent(xa.at[pl.ds(0, 15)], A2)
+    sqs[...] = to_row(square + jnp.where(y == 0, square1, 0.0), 128)
     for k, dev in enumerate(mp_peers):
         send(sqs, sq1.at[k], Q1, dev)
     sent(sq1, Q1)
-    wait_in(xa.at[0, 0, pl.ds(0, 3)], A1)
-    for dev in dp_peers:
-        send(xa.at[c, dp], xa.at[c, dp], A2, dev)
-    sent(xa.at[0, pl.ds(0, 15)], A2)
+    wait_in(xb.at[0, pl.ds(0, 15)], B1)
+    for dev in y_peers:
+        send(xb.at[y], xb.at[y], B2, dev)
+    sent(xb.at[pl.ds(0, 3)], B2)
     wait_in(sq1, Q1)
     total = sqs[...]
     for k in range(7):
         total = total + sq1[k]
     sq2[dp] = total
-    for dev in dp_peers:
-        send(sq2.at[dp], sq2.at[dp], Q2, dev)
+    over_dp(sq2.at[dp], Q2)
     sent(sq2.at[pl.ds(0, 15)], Q2)
-    wait_in(xb.at[0, 0, pl.ds(0, 15)], B1)
-    for dev in y_peers:
-        send(xb.at[c, y], xb.at[c, y], B2, dev)
-    sent(xb.at[0, pl.ds(0, 3)], B2)
-    need(temp, bhead)
+
+    need(temp)
     temp_col = to_col(temp[...], 256)
-    wait_in(xa.at[0, pl.ds(0, 15)], A2)
-    send(xa.at[c], xa.at[c], A3, sibling)
-    sent(xa.at[0], A3)
+    wait_in(bhs, HD)
+
+    def own_rows(yy, at, size):
+        return bhead[pl.ds(pl.multiple_of((2 * yy + c) * 512 + at, 256), size), :]
+
+    def gathered(first, buf_rows, at):
+        for yy in range(4):
+            rows = buf_rows(yy)
+            theirs, ours = mm(rows, bhs[yy, at : at + 256, :]), mm(rows, own_rows(yy, at, 256))
+            fresh = first and yy == 0
+            psib[...] = theirs if fresh else psib[...] + theirs
+            pown[...] = ours if fresh else pown[...] + ours
+
+    wait_in(xa.at[pl.ds(0, 15)], A2)
+    gathered(True, lambda yy: xa[:, :, yy * 256 : (yy + 1) * 256].reshape(256, 256), 0)
+    wait_in(xb.at[pl.ds(0, 3)], B2)
+    gathered(False, lambda yy: xb[yy].reshape(256, 256), 256)
+    send(psib, prcv, PX, sibling)
+    sent(psib, PX)
+    acc = pown[...]
     wait_in(sq2.at[pl.ds(0, 15)], Q2)
-    sums = sq2[:, 0:1, :]
-    sums = jnp.sum(
-        jnp.where((iota((16, 16, 128), 1) == iota((16, 16, 128), 2)), sums, 0.0),
-        axis=2, keepdims=True,
-    ).reshape(256, 1)
+    sums = spread_rows(sq2[...])
     row_scale = lax.rsqrt(sums * (1.0 / 4096.0) + EPS)
-
-
-    def head_a(cc, acc):
-        for yy in range(4):
-            rows = pl.ds(pl.multiple_of((2 * yy + cc) * 512, 256), 256)
-            part = mm(xa[cc, :, yy].reshape(256, 256), bhead[rows, :])
-            acc = part if acc is None else acc + part
-        return acc
-
-    def head_b(cc, acc):
-        for yy in range(4):
-            rows = pl.ds(pl.multiple_of((2 * yy + cc) * 512 + 256, 256), 256)
-            acc = acc + mm(xb[cc, yy].reshape(256, 256), bhead[rows, :])
-        return acc
-
-    acc = head_a(c, None)
-    wait_in(xb.at[0, pl.ds(0, 3)], B2)
-    send(xb.at[c], xb.at[c], B3, sibling)
-    sent(xb.at[0], B3)
-    acc = head_b(c, acc)
-    wait_in(xa.at[0], A3)
-    acc = head_a(1 - c, acc)
-    wait_in(xb.at[0], B3)
-    acc = head_b(1 - c, acc)
-
-    combined = temp_col * (acc * row_scale + slog[...])
+    wait_in(prcv, PX)
+    combined = temp_col * ((acc + prcv[...]) * row_scale + slog[...])
     peak = jnp.max(combined, axis=1, keepdims=True)
     lse = peak + jnp.log(jnp.sum(jnp.exp(combined - peak), axis=1, keepdims=True))
 
@@ -442,22 +522,36 @@
         pltpu.VMEM((8, 2, 16, 128), F32),
         pltpu.VMEM((7, 2, 16, 128), F32),
         pltpu.VMEM((8, 2, 16, 128), F32),
-        pltpu.VMEM((2, 16, 16, 1024), BF16),
-        pltpu.VMEM((8, 16, 8, d // 8), BF16),
-        pltpu.VMEM((8, 16, 8, d // 8), BF16),
-        pltpu.VMEM((2, 16, 4, 16, 256), BF16),
-        pltpu.VMEM((2, 4, 16, 16, 256), BF16),
-        pltpu.VMEM((7, 8, 128), F32),
-        pltpu.VMEM((16, 8, 128), F32),
-        pltpu.VMEM((8, 128), F32),
+        pltpu.VMEM((2, 2, 16, 16, 512), BF16),
+        pltpu.VMEM((2, 16, 8, 1024), BF16),
+        pltpu.VMEM((2, 16, 8, 1024), BF16),
+        pltpu.VMEM((2, 4, 128, 256), BF16),
+        pltpu.VMEM((8, 128, 256), BF16),
+        pltpu.VMEM((2, 16, 1024), BF16),
+        pltpu.VMEM((8, 16, 1024), BF16),
+        pltpu.VMEM((16, 16, 256), BF16),
+        pltpu.VMEM((15, 16, 256), BF16),
+        pltpu.VMEM((2, 128), F32),
+        pltpu.VMEM((16, 2, 128), F32),
+        pltpu.VMEM((256, 1024), BF16),
+        pltpu.VMEM((256, 1024), BF16),
+        pltpu.VMEM((16, 16, 1024), BF16),
+        pltpu.VMEM((4, 16, 16, 256), BF16),
+        pltpu.VMEM((4, 512, vs), BF16),
+        pltpu.VMEM((256, vs), F32),
+        pltpu.VMEM((256, vs), F32),
+        pltpu.VMEM((256, vs), F32),
+        pltpu.VMEM((7, 1, 128), F32),
+        pltpu.VMEM((16, 1, 128), F32),
+        pltpu.VMEM((1, 128), F32),
         pltpu.VMEM((2, 1, 256), F32),
         pltpu.VMEM((15, 1, 256), F32),
         pltpu.VMEM((7, 1, 256), F32),
         pltpu.VMEM((256, vs), F32),
-        pltpu.VMEM((8, 16, 128), F32),
+        pltpu.VMEM((16, 128), F32),
         pltpu.SemaphoreType.DMA((13 + 2 * WC + 3,)),
-        pltpu.SemaphoreType.DMA((31,)),
-        pltpu.SemaphoreType.DMA((31,)),
+        pltpu.SemaphoreType.DMA((35,)),
+        pltpu.SemaphoreType.DMA((35,)),
     ]
     return pl.pallas_call(
         kernel,

time: 63.8 us -> 60.3 us (0.945)
  Pallas kernels: 63 us -> 59.6 us
    pallas_call x1, Pallas kernels: 63 us -> 59.6 us  [per_device(): pl.pallas_call(kernel, name='decode_step', out_shape=jax.ShapeDtypeStruct...]
where the time goes in v3:
time: 60.3 us; the launch traced here: 60.2 us
  Pallas kernels  59.6 us (99%)
  local copies, waits for them, and re-layouts  0.66 us (1%)
    pallas_call x1, Pallas kernels, per_device(): pl.pallas_call(kernel, name='decode_step', out_shape=jax.ShapeDtypeStruct...  59.6 us

profile of v3, /device:TPU:1, one launch (start us, length us, event | category | flops | bytes accessed | tf_op | source)
XLA Modules:
  0.0 60.2 jit_solution(13884721751599230659)
XLA Ops:
  0.0 59.6 %decode_step.1 = f32[256,125]{1,0:T(8,128)S(1)} custom-call(bf16[16,4096]{1,0:T(8,128)(2,1)} %tokens_h.1, f32[1,4096]{1,0:T(1,128)} %bitcast.9, bf16[8,4096]{1,0:T(8,128)(2,1)} %bitcast.8, bf16[1,4096,896]{2,1,0:T(8,128)(2,1)} %w_gate_h.1, bf16[1,4096,896]{2,1,0:T(8,128)(2,1)} %w_up_h.1, bf16[1,896,4096]{2,1,0:T(8,128)(2,1)} %w_down_h.1, ...), custom_call_target="tpu_custom_call" | custom-call | tf_op jit(solution)/shard_map/decode_step/pallas_call | solution.py:556
  59.6 0.7 %copy.20 = f32[256,125]{1,0:T(8,128)} copy(f32[256,125]{1,0:T(8,128)S(1)} %decode_step.1) | data formatting | bytes 256000

commit v4 on v3

--- a/solution.py
+++ b/solution.py
@@ -25,11 +25,17 @@
 
 
 def to_col(row, rows):
+    if rows > 128:
+        parts = [to_col(row[:, i : i + 128], 128) for i in range(0, rows, 128)]
+        return jnp.concatenate(parts, axis=0)
     n = row.shape[1]
     return jnp.sum(jnp.where(eye(rows, n), row, 0.0), axis=1, keepdims=True)
 
 
 def to_row(col, cols):
+    if cols > 128:
+        parts = [to_row(col[i : i + 128], 128) for i in range(0, cols, 128)]
+        return jnp.concatenate(parts, axis=1)
     n = col.shape[0]
     return jnp.sum(jnp.where(eye(n, cols), col, 0.0), axis=0, keepdims=True)
 
@@ -47,9 +53,9 @@
     hidden_h, query_h, cache_h, new_h, len_h, sout_h, sgain_h, bhead_h, shead_h, temp_h,
     out_ref,
     tokens, norm_gain, router, w_gate, w_up, w_down, final_gain, routes,
-    hidden, query, cache, new, clen, sout, sgain, bhead, shead, temp,
-    xr, act, pbuf, prec, stbuf, sall, r1s, r1r, r2s, r2r, m1s, m1r, d2s, d2r, gs, gr, wh, wl,
-    xa, xb, bhs, psib, prcv, pown, sq1, sq2, sqs, lsend, l1, l2, slog, comb_s,
+    hidden, query, cache, new, clen, sout, sgain, shead, temp,
+    xr, gpart, upart, act, pbuf, prec, stbuf, sall, r1s, r1r, r2s, r2r, m1s, m1r, d2s, d2r, gs, gr, wh, wl,
+    xa, xb, bho, bht, bhs, psib, prcv, pown, sq1, sq2, sqs, lsend, l1, l2, slog, comb_s,
     lsem, bsem_s, bsem_r,
 ):
     dp = lax.axis_index("dp")
@@ -66,6 +72,12 @@
     dp_peers = [
         (dp_at(k // 4, k % 4), mp) for k in (1, 3, 4, 12, 5, 7, 13, 15, 2, 8, 6, 14, 9, 11, 10)
     ]
+    def to_x(kx):
+        return (dp_at(0, kx), mp)
+
+    def to_z(kz):
+        return (dp_at(kz, 0), mp)
+
     mp_peers = [(dp, lax.rem(mp + k, 8)) for k in range(1, 8)]
     y_peers = [(dp, lax.rem(y + k, 4) * 2 + c) for k in (1, 3, 2)]
     sibling = (dp, y * 2 + 1 - c)
@@ -88,8 +100,14 @@
     def sent(ref, phase):
         pending.append((ref, phase))
 
-    (XA, XB, PR, ST, SA, SB, S3, A2, B1, B2, HD, PX, Q1, Q2, L1, L2, G, M1, D2, R2, R1) = range(21)
-    X1, Y1 = 21, 27
+    (XC, XD, X2) = (38, 39, 39)
+    (XA, XB, PR, ST, SA, SB, S3, A2, B2, HD, PX, Q1, Q2, L1, L2, G, M1, D2, R2, R1) = range(20)
+    X1, Y1, B1 = 20, 26, 34
+
+    barrier = pltpu.get_barrier_semaphore()
+    greeted = [to_x(k) for k in (1, 3, 2)] + [to_z(k) for k in (1, 3, 2)] + mp_peers
+    for dev in greeted:
+        pl.semaphore_signal(barrier, inc=1, device_id=dev, device_id_type=pl.DeviceIdType.MESH)
 
     pairs = [
         (tokens_h, tokens), (norm_gain_h, norm_gain), (routes_h, routes), (router_h, router),
@@ -97,7 +115,7 @@
         (hidden_h, hidden), (sgain_h, sgain),
         (final_gain_h, final_gain), (temp_h, temp),
     ]
-    late = [(w_down_h.at[0], w_down), (shead_h, shead), (bhead_h, bhead)]
+    late = [(w_down_h.at[0], w_down), (shead_h, shead)]
     copies = {}
 
     def fetch(src, dst, n):
@@ -109,9 +127,6 @@
     for src, dst in pairs:
         copies[id(dst)] = fetch(src, dst, n)
         n += 1
-    barrier = pltpu.get_barrier_semaphore()
-    for dev in dp_peers + mp_peers:
-        pl.semaphore_signal(barrier, inc=1, device_id=dev, device_id_type=pl.DeviceIdType.MESH)
     wcopies = []
     kw = w_gate.shape[0] // WC
     for i in range(WC):
@@ -123,6 +138,17 @@
         copies[id(dst)] = fetch(src, dst, n)
         n += 1
 
+    for parity, dst in ((c, bho), (1 - c, bht)):
+        for yy in range(4):
+            for at in range(2):
+                rows = pl.ds(pl.multiple_of((2 * yy + parity) * 512 + at * 256, 256), 256)
+                pltpu.make_async_copy(
+                    bhead_h.at[rows], dst.at[at, pl.ds(yy * 256, 256)],
+                    lsem.at[n if dst is bho else n + 1],
+                ).start()
+    copies[id(bho)] = pltpu.make_async_copy(bho, bho, lsem.at[n])
+    copies[id(bht)] = pltpu.make_async_copy(bht, bht, lsem.at[n + 1])
+
     def need(*refs):
         with jax.named_scope("need"):
             for r in refs:
@@ -152,9 +178,47 @@
     select = jnp.where(
         (hit_row > 0.5) & (rank_row == iota((8, 128), 0).astype(F32)), 1.0, 0.0
     )[:, :16].astype(BF16)
-    half = xr.shape[3]
-    xr[0, 0] = mm(select, normed[:, :half]).astype(BF16)
-    xr[1, 0] = mm(select, normed[:, half:]).astype(BF16)
+    quarter = xr.shape[4]
+    for colour in range(2):
+        for chunk in range(2):
+            at = (2 * colour + chunk) * quarter
+            xr[chunk, colour, 0] = mm(select, normed[:, at : at + quarter]).astype(BF16)
+
+    with jax.named_scope("barrier"):
+        pl.semaphore_wait(barrier, len(greeted))
+
+    def spread(buf, base, pa, pb):
+        for k in (1, 3, 2):
+            send(buf(0, 0, 0, 0), buf(0, 0, 0, k), base + k, to_x(k))
+            send(buf(1, 0, 0, 0), buf(1, 0, k, 0), base + 3 + k, to_z(k))
+        for k in (1, 3, 2):
+            send(buf(0, 0, 0, 0), buf(0, 0, k, 0), pa, to_z(k))
+            send(buf(1, 0, 0, 0), buf(1, 0, 0, k), pb, to_x(k))
+
+    def forward(buf, base, pa, pb):
+        for k in (1, 3, 2):
+            wait_in(buf(0, k, 0, 0), base + k)
+            for kz in (1, 3, 2):
+                send(buf(0, k, 0, 0), buf(0, k, kz, 0), pa, to_z(kz))
+            wait_in(buf(1, 4 * k, 0, 0), base + 3 + k)
+            for kx in (1, 3, 2):
+                send(buf(1, 4 * k, 0, 0), buf(1, 4 * k, 0, kx), pb, to_x(kx))
+            sent(buf(0, 0, 0, 0), base + k)
+            sent(buf(0, 0, 0, 0), base + 3 + k)
+
+    def xblock0(colour, place, az, ax):
+        return xr.at[0, colour, place + 4 * az + ax]
+
+    def xblock1(colour, place, az, ax):
+        return xr.at[1, colour, place + 4 * az + ax]
+
+    def sblock(colour, place, az, ax):
+        return sall.at[c, colour, dp_at(4 - place // 4, 4 - place % 4)]
+
+    for block, base, pa, pb in ((xblock0, X1, XA, XB), (xblock1, X2, XC, XD)):
+        spread(block, base, pa, pb)
+        sent(xr.at[0, 0, pl.ds(0, 12)], pa)
+        sent(xr.at[0, 0, pl.ds(0, 12)], pb)
 
     need(query, cache, new, clen, sout)
     len_col = to_col(clen[...].astype(F32), 16).astype(jnp.int32)
@@ -178,49 +242,12 @@
         proj = mm(att.astype(BF16), sout[m])
         for e in range(8):
             pbuf[e, m] = proj[:, e * 128 : (e + 1) * 128]
-    with jax.named_scope("barrier"):
-        pl.semaphore_wait(barrier, 22)
-
-    def to_x(kx):
-        return (dp_at(0, kx), mp)
-
-    def to_z(kz):
-        return (dp_at(kz, 0), mp)
-
-    def spread(buf, base, pa, pb):
-        for k in (1, 3, 2):
-            send(buf(0, 0, 0, 0), buf(0, 0, 0, k), base + k, to_x(k))
-            send(buf(1, 0, 0, 0), buf(1, 0, k, 0), base + 3 + k, to_z(k))
-        for k in (1, 3, 2):
-            send(buf(0, 0, 0, 0), buf(0, 0, k, 0), pa, to_z(k))
-            send(buf(1, 0, 0, 0), buf(1, 0, 0, k), pb, to_x(k))
-
-    def forward(buf, base, pa, pb):
-        for k in (1, 3, 2):
-            wait_in(buf(0, k, 0, 0), base + k)
-            for kz in (1, 3, 2):
-                send(buf(0, k, 0, 0), buf(0, k, kz, 0), pa, to_z(kz))
-            wait_in(buf(1, 4 * k, 0, 0), base + 3 + k)
-            for kx in (1, 3, 2):
-                send(buf(1, 4 * k, 0, 0), buf(1, 4 * k, 0, kx), pb, to_x(kx))
-            sent(buf(0, 0, 0, 0), base + k)
-            sent(buf(0, 0, 0, 0), base + 3 + k)
-
-    def xblock(colour, place, az, ax):
-        return xr.at[colour, place + 4 * az + ax]
-
-    def sblock(colour, place, az, ax):
-        return sall.at[c, colour, dp_at(4 - place // 4, 4 - place % 4)]
-
-    spread(xblock, X1, XA, XB)
-    sent(xr.at[0, pl.ds(0, 12)], XA)
-    sent(xr.at[1, pl.ds(0, 12)], XB)
-
     for k, dev in enumerate(mp_peers):
         send(pbuf.at[dev[1]], prec.at[k], PR, dev)
     sent(prec, PR)
 
-    forward(xblock, X1, XA, XB)
+    forward(xblock0, X1, XA, XB)
+    forward(xblock1, X2, XC, XD)
 
     need(router)
     logits = nt(normed, router[...])
@@ -251,6 +278,42 @@
     for dev in mp_peers:
         send(stbuf.at[mp], stbuf.at[mp], ST, dev)
     sent(stbuf.at[pl.ds(0, 7)], ST)
+    with jax.named_scope("weights"):
+        for cp in wcopies:
+            cp.wait()
+
+    def up_tile(chunk, col, width):
+        cols = pl.ds(col, width)
+        g = u = None
+        for colour in range(2):
+            rows = xr[chunk, colour].reshape(128, quarter)
+            depth = pl.ds((2 * colour + chunk) * quarter, quarter)
+            dg, du = mm(rows, w_gate[depth, cols]), mm(rows, w_up[depth, cols])
+            g, u = (dg, du) if g is None else (g + dg, u + du)
+        if chunk == 0:
+            gpart[:, cols] = g
+            upart[:, cols] = u
+        else:
+            g, u = g + gpart[:, cols], u + upart[:, cols]
+            act[:, cols] = (g / (1.0 + jnp.exp(-g)) * u).astype(BF16)
+
+    ff = w_gate.shape[1]
+    full = ff // 256
+
+    def up_chunk(chunk, pa, pb):
+        wait_in(xr.at[0, 0, pl.ds(0, 12)], pa)
+        wait_in(xr.at[0, 0, pl.ds(0, 12)], pb)
+
+        def up_body(i, carry):
+            up_tile(chunk, pl.multiple_of(i * 256, 256), 256)
+            return carry
+
+        lax.fori_loop(0, full, up_body, 0)
+        if ff % 256:
+            up_tile(chunk, full * 256, ff % 256)
+
+    up_chunk(0, XA, XB)
+
     wait_in(stbuf.at[pl.ds(0, 7)], ST)
     sq_sum = jnp.zeros((16, 1), F32)
     for e in range(8):
@@ -263,40 +326,15 @@
         cols = slice(e * 128, (e + 1) * 128)
         inner = slice(e % 4 * 128, (e % 4 + 1) * 128)
         sall[c, e // 4, dp, :, inner] = (stbuf[e, c] * inv * g[:, cols]).astype(BF16)
-    need(bhead)
-    for yy in range(4):
-        rows = pl.ds(pl.multiple_of((2 * yy + 1 - c) * 512, 512), 512)
-        send(bhead.at[rows], bhs.at[yy], HD, sibling)
+    need(bht)
+    send(bht, bhs, HD, sibling)
     sent(bhs, HD)
 
-    wait_in(xr.at[0, pl.ds(0, 12)], XA)
-    wait_in(xr.at[1, pl.ds(0, 12)], XB)
     spread(sblock, Y1, SA, SB)
     sent(sall.at[0, 0, pl.ds(0, 12)], SA)
     sent(sall.at[0, 1, pl.ds(0, 12)], SB)
-    with jax.named_scope("weights"):
-        for cp in wcopies:
-            cp.wait()
-
-    def up_tile(col, width):
-        cols = pl.ds(col, width)
-        lo, hi = xr[0].reshape(128, half), xr[1].reshape(128, half)
-        g = mm(lo, w_gate[:half, cols]) + mm(hi, w_gate[half:, cols])
-        u = mm(lo, w_up[:half, cols]) + mm(hi, w_up[half:, cols])
-        act[:, pl.ds(col, width)] = (g / (1.0 + jnp.exp(-g)) * u).astype(BF16)
-
-    ff = w_gate.shape[1]
-    full = ff // 256
-
-    def up_body(i, carry):
-        up_tile(pl.multiple_of(i * 256, 256), 256)
-        return carry
-
-    lax.fori_loop(0, full, up_body, 0)
-    if ff % 256:
-        up_tile(full * 256, ff % 256)
-
-    forward(sblock, Y1, SA, SB)
+    up_chunk(1, XC, XD)
+
     need(w_down)
     for core in range(2):
         phase = R1 if core == 0 else Y1 + 7
@@ -351,19 +389,6 @@
         wh[:, e * 128 : (e + 1) * 128] = high
         wl[:, e * 128 : (e + 1) * 128] = (w - high.astype(F32)).astype(BF16)
 
-    wait_in(sall.at[0, 0, pl.ds(0, 12)], SA)
-    wait_in(sall.at[0, 1, pl.ds(0, 12)], SB)
-    send(sall.at[c], sall.at[c], S3, sibling)
-    sent(sall.at[0], S3)
-    need(shead)
-    wait_in(sall.at[0], S3)
-    for m in range(2):
-        head = shead[:, m, :]
-        part = nt(sall[m, 0].reshape(256, 512), head[:, :512]) + nt(
-            sall[m, 1].reshape(256, 512), head[:, 512:]
-        )
-        slog[...] = part if m == 0 else ALPHA * (slog[...] - part)
-
     need(final_gain)
 
     def over_dp(buf, phase):
@@ -392,13 +417,14 @@
                 def _():
                     send(m1s.at[core], m1r.at[mp], M1, dev)
 
-    mix(0)
     wait_in(r2r.at[pl.ds(0, 7)], R2)
     rows = r2r[...].reshape(1024, 256)
     d2s[...] = (mm(wh[...], rows) + mm(wl[...], rows)).astype(BF16).reshape(16, 16, 256)
     for k, dev in enumerate(dp_peers):
         send(d2s.at[dev[0]], d2r.at[k], D2, dev)
     sent(d2r, D2)
+    forward(sblock, Y1, SA, SB)
+    mix(0)
     mix(1)
     sent(m1r.at[pl.ds(0, 7)], M1)
     m1r[mp] = m1s[c]
@@ -408,9 +434,14 @@
     state = tokens[:, cols].astype(F32) + d2s[dp].astype(F32)
     for k in range(15):
         state = state + d2r[k].astype(F32)
-    xb[y, dp] = (state * final_gain[:, cols]).astype(BF16)
-    over_dp(xb.at[y, dp], B1)
-    sent(xb.at[0, pl.ds(0, 15)], B1)
+    y_cols = pl.ds(pl.multiple_of(y * 256, 256), 256)
+    xb[dp, :, y_cols] = (state * final_gain[:, cols]).astype(BF16)
+    block = xb.at[dp, :, y_cols]
+    for kz in range(4):
+        for kx in (0, 1, 3, 2):
+            if kz or kx:
+                send(block, block, B1 + kz, (dp_at(kz, kx), mp))
+        sent(xb.at[pl.ds(0, 4 if kz else 3), :, pl.ds(0, 256)], B1 + kz)
     square = jnp.sum(state * state, axis=1, keepdims=True)
 
     wait_in(m1r.at[pl.ds(0, 7)], M1)
@@ -429,10 +460,19 @@
     for k, dev in enumerate(mp_peers):
         send(sqs, sq1.at[k], Q1, dev)
     sent(sq1, Q1)
-    wait_in(xb.at[0, pl.ds(0, 15)], B1)
-    for dev in y_peers:
-        send(xb.at[y], xb.at[y], B2, dev)
-    sent(xb.at[pl.ds(0, 3)], B2)
+
+    def group(kz):
+        wait_in(xb.at[pl.ds(0, 4 if kz else 3), :, pl.ds(0, 256)], B1 + kz)
+        blocks = xb.at[pl.ds(4 * zs[(4 - kz) % 4], 4), :, y_cols]
+        for dev in y_peers:
+            send(blocks, blocks, B2, dev)
+
+    wait_in(sall.at[0, 0, pl.ds(0, 12)], SA)
+    wait_in(sall.at[0, 1, pl.ds(0, 12)], SB)
+    send(sall.at[c], sall.at[c], S3, sibling)
+    sent(sall.at[0], S3)
+
+    group(0)
     wait_in(sq1, Q1)
     total = sqs[...]
     for k in range(7):
@@ -440,29 +480,33 @@
     sq2[dp] = total
     over_dp(sq2.at[dp], Q2)
     sent(sq2.at[pl.ds(0, 15)], Q2)
-
-    need(temp)
+    group(1)
+    group(3)
+    group(2)
+    sent(xb.at[:, :, pl.ds(0, 768)], B2)
+
+    need(shead)
+    wait_in(sall.at[0], S3)
+    for m in range(2):
+        head = shead[:, m, :]
+        part = nt(sall[m, 0].reshape(256, 512), head[:, :512]) + nt(
+            sall[m, 1].reshape(256, 512), head[:, 512:]
+        )
+        slog[...] = part if m == 0 else ALPHA * (slog[...] - part)
+
+    need(temp, bho)
     temp_col = to_col(temp[...], 256)
     wait_in(bhs, HD)
-
-    def own_rows(yy, at, size):
-        return bhead[pl.ds(pl.multiple_of((2 * yy + c) * 512 + at, 256), size), :]
-
-    def gathered(first, buf_rows, at):
-        for yy in range(4):
-            rows = buf_rows(yy)
-            theirs, ours = mm(rows, bhs[yy, at : at + 256, :]), mm(rows, own_rows(yy, at, 256))
-            fresh = first and yy == 0
-            psib[...] = theirs if fresh else psib[...] + theirs
-            pown[...] = ours if fresh else pown[...] + ours
-
     wait_in(xa.at[pl.ds(0, 15)], A2)
-    gathered(True, lambda yy: xa[:, :, yy * 256 : (yy + 1) * 256].reshape(256, 256), 0)
-    wait_in(xb.at[pl.ds(0, 3)], B2)
-    gathered(False, lambda yy: xb[yy].reshape(256, 256), 256)
+    rows = xa[...].reshape(256, 1024)
+    psib[...] = mm(rows, bhs[0])
+    pown[...] = mm(rows, bho[0])
+    wait_in(xb.at[:, :, pl.ds(0, 768)], B2)
+    rows = xb[...].reshape(256, 1024)
+    psib[...] += mm(rows, bhs[1])
     send(psib, prcv, PX, sibling)
     sent(psib, PX)
-    acc = pown[...]
+    acc = pown[...] + mm(rows, bho[1])
     wait_in(sq2.at[pl.ds(0, 15)], Q2)
     sums = spread_rows(sq2[...])
     row_scale = lax.rsqrt(sums * (1.0 / 4096.0) + EPS)
@@ -491,11 +535,10 @@
     for k, dev in enumerate(mp_peers):
         send(lsend.at[1], l2.at[k], L2, dev)
     sent(l2, L2)
+    for ref, phase in pending:
+        rcopy(ref, ref, phase, sibling).wait_send()
     wait_in(l2, L2)
     out_ref[...] = combined - to_col(merge(row, l2, 7), 256)
-
-    for ref, phase in pending:
-        rcopy(ref, ref, phase, sibling).wait_send()
 
 
 def per_device(
@@ -515,9 +558,11 @@
     def like(a, drop=0):
         return pltpu.VMEM(a.shape[drop:], a.dtype)
 
-    fetched = [like(a, 1 if k in (3, 4, 5) else 0) for k, a in enumerate(args)]
+    fetched = [like(a, 1 if k in (3, 4, 5) else 0) for k, a in enumerate(args) if k != 15]
     scratch = fetched + [
-        pltpu.VMEM((2, 16, 8, d // 2), BF16),
+        pltpu.VMEM((2, 2, 16, 8, d // 4), BF16),
+        pltpu.VMEM((128, w_gate.shape[2]), F32),
+        pltpu.VMEM((128, w_gate.shape[2]), F32),
         pltpu.VMEM((128, w_gate.shape[2]), BF16),
         pltpu.VMEM((8, 2, 16, 128), F32),
         pltpu.VMEM((7, 2, 16, 128), F32),
@@ -536,8 +581,10 @@
         pltpu.VMEM((256, 1024), BF16),
         pltpu.VMEM((256, 1024), BF16),
         pltpu.VMEM((16, 16, 1024), BF16),
-        pltpu.VMEM((4, 16, 16, 256), BF16),
-        pltpu.VMEM((4, 512, vs), BF16),
+        pltpu.VMEM((16, 16, 1024), BF16),
+        pltpu.VMEM((2, 1024, vs), BF16),
+        pltpu.VMEM((2, 1024, vs), BF16),
+        pltpu.VMEM((2, 1024, vs), BF16),
         pltpu.VMEM((256, vs), F32),
         pltpu.VMEM((256, vs), F32),
         pltpu.VMEM((256, vs), F32),
@@ -549,9 +596,9 @@
         pltpu.VMEM((7, 1, 256), F32),
         pltpu.VMEM((256, vs), F32),
         pltpu.VMEM((16, 128), F32),
-        pltpu.SemaphoreType.DMA((13 + 2 * WC + 3,)),
-        pltpu.SemaphoreType.DMA((35,)),
-        pltpu.SemaphoreType.DMA((35,)),
+        pltpu.SemaphoreType.DMA((13 + 2 * WC + 4,)),
+        pltpu.SemaphoreType.DMA((46,)),
+        pltpu.SemaphoreType.DMA((46,)),
     ]
     return pl.pallas_call(
         kernel,

time: 60.3 us -> 56.5 us (0.937)
  Pallas kernels: 59.6 us -> 55.7 us
    pallas_call x1, Pallas kernels: 59.6 us -> 55.7 us  [per_device(): pl.pallas_call(kernel, name='decode_step', out_shape=jax.ShapeDtypeStruct...]
where the time goes in v4:
time: 56.5 us; the launch traced here: 56.4 us
  Pallas kernels  55.7 us (99%)
  local copies, waits for them, and re-layouts  0.66 us (1%)
    pallas_call x1, Pallas kernels, per_device(): pl.pallas_call(kernel, name='decode_step', out_shape=jax.ShapeDtypeStruct...  55.7 us

profile of v4, /device:TPU:1, one launch (start us, length us, event | category | flops | bytes accessed | tf_op | source)
XLA Modules:
  0.0 56.4 jit_solution(13991582344441964555)
XLA Ops:
  0.0 55.7 %decode_step.1 = f32[256,125]{1,0:T(8,128)S(1)} custom-call(bf16[16,4096]{1,0:T(8,128)(2,1)} %tokens_h.1, f32[1,4096]{1,0:T(1,128)} %bitcast.9, bf16[8,4096]{1,0:T(8,128)(2,1)} %bitcast.8, bf16[1,4096,896]{2,1,0:T(8,128)(2,1)} %w_gate_h.1, bf16[1,4096,896]{2,1,0:T(8,128)(2,1)} %w_up_h.1, bf16[1,896,4096]{2,1,0:T(8,128)(2,1)} %w_down_h.1, ...), custom_call_target="tpu_custom_call" | custom-call | tf_op jit(solution)/shard_map/decode_step/pallas_call | solution.py:603
  55.7 0.7 %copy.20 = f32[256,125]{1,0:T(8,128)} copy(f32[256,125]{1,0:T(8,128)S(1)} %decode_step.1) | data formatting | bytes 256000

commit v5 on v4

--- a/solution.py
+++ b/solution.py
@@ -70,7 +70,7 @@
         return zs[kz % 4] * 4 + xs[kx % 4]
 
     dp_peers = [
-        (dp_at(k // 4, k % 4), mp) for k in (1, 3, 4, 12, 5, 7, 13, 15, 2, 8, 6, 14, 9, 11, 10)
+        (dp_at(k // 4, k % 4), mp) for k in (10, 9, 11, 6, 14, 2, 8, 5, 7, 13, 15, 1, 3, 4, 12)
     ]
     def to_x(kx):
         return (dp_at(0, kx), mp)
@@ -78,8 +78,8 @@
     def to_z(kz):
         return (dp_at(kz, 0), mp)
 
-    mp_peers = [(dp, lax.rem(mp + k, 8)) for k in range(1, 8)]
-    y_peers = [(dp, lax.rem(y + k, 4) * 2 + c) for k in (1, 3, 2)]
+    mp_peers = [(dp, lax.rem(mp + k, 8)) for k in (4, 3, 5, 2, 6, 1, 7)]
+    y_peers = [(dp, lax.rem(y + k, 4) * 2 + c) for k in (2, 1, 3)]
     sibling = (dp, y * 2 + 1 - c)
 
     def rcopy(src, dst, phase, dev):
@@ -188,20 +188,20 @@
         pl.semaphore_wait(barrier, len(greeted))
 
     def spread(buf, base, pa, pb):
-        for k in (1, 3, 2):
+        for k in (2, 1, 3):
             send(buf(0, 0, 0, 0), buf(0, 0, 0, k), base + k, to_x(k))
             send(buf(1, 0, 0, 0), buf(1, 0, k, 0), base + 3 + k, to_z(k))
-        for k in (1, 3, 2):
+        for k in (2, 1, 3):
             send(buf(0, 0, 0, 0), buf(0, 0, k, 0), pa, to_z(k))
             send(buf(1, 0, 0, 0), buf(1, 0, 0, k), pb, to_x(k))
 
     def forward(buf, base, pa, pb):
         for k in (1, 3, 2):
             wait_in(buf(0, k, 0, 0), base + k)
-            for kz in (1, 3, 2):
+            for kz in (2, 1, 3):
                 send(buf(0, k, 0, 0), buf(0, k, kz, 0), pa, to_z(kz))
             wait_in(buf(1, 4 * k, 0, 0), base + 3 + k)
-            for kx in (1, 3, 2):
+            for kx in (2, 1, 3):
                 send(buf(1, 4 * k, 0, 0), buf(1, 4 * k, 0, kx), pb, to_x(kx))
             sent(buf(0, 0, 0, 0), base + k)
             sent(buf(0, 0, 0, 0), base + 3 + k)
@@ -304,11 +304,8 @@
         wait_in(xr.at[0, 0, pl.ds(0, 12)], pa)
         wait_in(xr.at[0, 0, pl.ds(0, 12)], pb)
 
-        def up_body(i, carry):
-            up_tile(chunk, pl.multiple_of(i * 256, 256), 256)
-            return carry
-
-        lax.fori_loop(0, full, up_body, 0)
+        for i in range(full):
+            up_tile(chunk, i * 256, 256)
         if ff % 256:
             up_tile(chunk, full * 256, ff % 256)
 
@@ -358,7 +355,7 @@
                 def _():
                     r2r[mp] = second
 
-        for k in (1, 3, 4, 12, 5, 7, 13, 15, 2, 8, 6, 14, 9, 11, 10):
+        for k in (10, 9, 11, 6, 14, 2, 8, 5, 7, 13, 15, 1, 3, 4, 12):
             send(r1s.at[core, k], r1r.at[core, k], phase, (dp_at(4 - k // 4, 4 - k % 4), mp))
         sent(r1r.at[0, pl.ds(0, 15)], phase)
     sent(r2r.at[pl.ds(0, 7)], R2)

time: 56.5 us -> 54.6 us (0.966)
  Pallas kernels: 55.7 us -> 53.8 us
    pallas_call x1, Pallas kernels: 55.7 us -> 53.8 us  [per_device(): pl.pallas_call(kernel, name='decode_step', out_shape=jax.ShapeDtypeStruct...]
where the time goes in v5:
time: 54.6 us; the launch traced here: 54.5 us
  Pallas kernels  53.8 us (99%)
  local copies, waits for them, and re-layouts  0.66 us (1%)
    pallas_call x1, Pallas kernels, per_device(): pl.pallas_call(kernel, name='decode_step', out_shape=jax.ShapeDtypeStruct...  53.8 us

profile of v5, /device:TPU:1, one launch (start us, length us, event | category | flops | bytes accessed | tf_op | source)
XLA Modules:
  0.0 54.5 jit_solution(901376080416333574)
XLA Ops:
  0.0 53.8 %decode_step.1 = f32[256,125]{1,0:T(8,128)S(1)} custom-call(bf16[16,4096]{1,0:T(8,128)(2,1)} %tokens_h.1, f32[1,4096]{1,0:T(1,128)} %bitcast.9, bf16[8,4096]{1,0:T(8,128)(2,1)} %bitcast.8, bf16[1,4096,896]{2,1,0:T(8,128)(2,1)} %w_gate_h.1, bf16[1,4096,896]{2,1,0:T(8,128)(2,1)} %w_up_h.1, bf16[1,896,4096]{2,1,0:T(8,128)(2,1)} %w_down_h.1, ...), custom_call_target="tpu_custom_call" | custom-call | tf_op jit(solution)/shard_map/decode_step/pallas_call | solution.py:600
  53.8 0.7 %copy.20 = f32[256,125]{1,0:T(8,128)} copy(f32[256,125]{1,0:T(8,128)S(1)} %decode_step.1) | data formatting | bytes 256000
